TPU v7x, 128 devices: a whole 4x4x4 slice. The times are simulated.
128 devices in a mesh: freq: 64 (over x, y, z_hi, core), depth: 2 (over z_lo).
Axes of the slice: x: 4, y: 4, z: 4 (z_hi: 2, z_lo: 2; z = z_hi * 2 + z_lo), core: 2. Of those that a mesh axis runs over, the one named last changes fastest.
Arguments:
- pressure_field: bfloat16 [8192, 16384], P('depth', 'freq'), may hold values from -6 to 6
- block_main: bfloat16 [8192, 3, 2, 128], P('depth'), may hold values from -0.15625 to 0.15625
- block_coupled: bfloat16 [8192, 3, 2, 128], P('depth'), may hold values from -0.15625 to 0.15625
- coupling: float32 [16384], P('freq'), may hold values from -3 to 3
- frequencies: float32 [8192], replicated, may hold values from 1 to 1024
- receivers: int32 [512], replicated, may hold values from 0 to 8191
- floors: int32 [4], replicated, may hold values from 2048 to 8191
Outputs:
- series: float32 [512, 2048], P('depth', 'freq')
Inputs may be any that keep to these rules, and one draw needn't show every extreme that they name: `receivers`: any depth cells, repeats possible.
All inputs are finite; a program needn't handle non-finite values.
Results may differ from a plain program's by a relative error of at most 0.0061.
Values may be sent and summed in bfloat16 or wider, within the bound.
No kernel may reach another device: no remote copies, remote signals or barrier semaphores. Data moves between devices by JAX's collectives and lax.ppermute only.
A program may use at most 256 MiB of HBM per device.

v0:
```python
import math

import jax
import jax.numpy as jnp
from jax import lax
from jax.sharding import PartitionSpec as P

NT = 2048
STEPS = 4


def padded_2(cells, sides, width):
    for axis, dim in sides:
        count = lax.axis_size(axis)
        ends = count - 1
        head = lax.slice_in_dim(cells, 0, width, axis=dim)
        tail = lax.slice_in_dim(cells, cells.shape[dim] - width, cells.shape[dim], axis=dim)
        cells = jnp.concatenate(
            [
                lax.ppermute(tail, axis, [(i, (i + 1) % count) for i in range(ends)]),
                cells,
                lax.ppermute(head, axis, [((i + 1) % count, i) for i in range(ends)]),
            ],
            axis=dim,
        )
    return cells


def in_blocks(x, dim, size):
    before, after = (x.shape[:dim], x.shape[dim + 1 :])
    return jnp.moveaxis(x.reshape(*before, size, -1, *after), dim, 0)


def summed_on_arrival(x, axis, dim):
    parts = in_blocks(x, dim, lax.axis_size(axis))
    arrived = lax.all_to_all(parts, axis, split_axis=0, concat_axis=0, tiled=True)
    return arrived.astype(jnp.float32).sum(axis=0)


def summed_on_arrival_2(x, axis, dim):
    parts = in_blocks(x, dim, lax.axis_size(axis))
    arrived = lax.all_to_all(parts, axis, split_axis=0, concat_axis=0, tiled=True)
    return arrived.sum(axis=0)


def times_unit(values):
    column = lax.broadcasted_iota(jnp.int32, values.shape, 1)
    upper = jnp.roll(values, -1, axis=1)
    lower = jnp.roll(values, 1, axis=1)
    return jnp.where(column % 2 == 0, -upper, lower)


def order_blocks(blocks, block_count, block_size):
    shaped = blocks.reshape(block_count, block_size, 3, 2, block_size)
    return shaped.transpose(0, 2, 3, 1, 4).reshape(block_count, 3, 2 * block_size, block_size)


def apply_blocks(ordered, padded, block_count, block_size):
    width = padded.shape[1]
    stacked = padded.reshape(block_count + 2, block_size, width)
    product = jnp.zeros((block_count, 2 * block_size, width), jnp.float32)
    for offset in range(3):
        product = product + jnp.einsum(
            "bij,bjc->bic",
            ordered[:, offset],
            stacked[offset : offset + block_count],
            preferred_element_type=jnp.float32,
        )
    real_part = product[:, :block_size].reshape(block_count * block_size, width)
    imag_part = product[:, block_size:].reshape(block_count * block_size, width)
    return real_part + times_unit(imag_part)


def make_basis(freq_values, sample_times):
    phase = jnp.mod(freq_values[:, None] * sample_times[None, :], jnp.float32(NT)) / jnp.float32(NT)
    angle = 2.0 * math.pi * phase
    stacked = jnp.stack([jnp.cos(angle), -jnp.sin(angle)], axis=1)
    return stacked.reshape(2 * freq_values.shape[0], sample_times.shape[0]).astype(jnp.bfloat16)


def local(pressure_field, block_main, block_coupled, coupling, frequencies, receivers, floors):
    rows_here = pressure_field.shape[0]
    block_size = block_main.shape[3]
    block_count = rows_here // block_size
    main_blocks = order_blocks(block_main, block_count, block_size)
    side_blocks = order_blocks(block_coupled, block_count, block_size)
    width = pressure_field.shape[1]
    column = jnp.arange(width, dtype=jnp.int32)
    even_weight = jnp.take(coupling, column - column % 2)
    odd_weight = jnp.take(coupling, column - column % 2 + 1)
    first_row = lax.axis_index("depth") * rows_here
    depth_index = first_row + jnp.arange(rows_here, dtype=jnp.int32)
    columns = pressure_field
    for step in range(STEPS):
        padded = padded_2(columns, (("depth", 0),), block_size)
        coupled = apply_blocks(side_blocks, padded, block_count, block_size)
        combined = (
            apply_blocks(main_blocks, padded, block_count, block_size)
            + even_weight[None, :] * coupled
            + odd_weight[None, :] * times_unit(coupled)
        )
        damping = jnp.where(depth_index >= floors[step], 0.5, 1.0).astype(jnp.float32)
        columns = (damping[:, None] * combined).astype(jnp.bfloat16)
    local_index = receivers - first_row
    selector = (local_index[:, None] == jnp.arange(rows_here, dtype=jnp.int32)[None, :]).astype(
        jnp.bfloat16
    )
    picked = jnp.dot(selector, columns, preferred_element_type=jnp.float32).astype(jnp.bfloat16)
    freq_here = columns.shape[1] // 2
    total_freq = frequencies.shape[0]
    factor = 1.0 / math.sqrt(total_freq)
    freq_values = lax.dynamic_slice_in_dim(
        frequencies, lax.axis_index("freq") * freq_here, freq_here, 0
    )
    basis_table = make_basis(freq_values, jnp.arange(NT, dtype=jnp.float32))
    owned_rows = summed_on_arrival(
        picked.astype(jnp.float32).astype(jnp.bfloat16), "depth", 0
    ).astype(jnp.bfloat16)
    owner_partial = jnp.dot(owned_rows, basis_table, preferred_element_type=jnp.float32)
    summed = summed_on_arrival_2(owner_partial, "freq", 1)
    return summed * factor


def solution(mesh):
    in_specs = (
        P("depth", "freq"),
        P("depth", None, None, None),
        P("depth", None, None, None),
        P("freq"),
        P(),
        P(),
        P(),
    )
    out_specs = P("depth", "freq")
    return jax.shard_map(local, mesh=mesh, in_specs=in_specs, out_specs=out_specs, check_vma=False)
```

profile of v0, /device:TPU:0, one launch (start us, length us, event | category | flops | bytes accessed | tf_op | source)
XLA Modules:
  0.0 525.7 jit_solution(9903431670786091757)
XLA Ops:
  0.9 3.9 collective-permute-start
  11.3 4.6 copy.23
  16.0 6.9 %copy.22 = bf16[32,128,3,2,128]{4,1,3,0,2:T(8,128)(2,1)S(1)} copy(bf16[32,128,3,2,128]{4,3,2,1,0:T(2,128)(2,1)} %bitcast.287) | data formatting | bytes 12582912 | tf_op jit(solution)/shard_map/reshape | solution.py:54
  23.0 5.1 fusion.93
  28.2 4.6 fusion.82
  41.5 5.8 %cosine_convert_fusion = (bf16[128,1,2048]{2,0,1:T(8,128)(2,1)}, bf16[128,1,2048]{2,0,1:T(8,128)(2,1)}) fusion(f32[128]{0:T(128)S(1)} %dynamic_slice.3), kind=kLoop, calls=%fused_computation.154 | loop fusion | flops 2883584 | bytes 1049088 | tf_op jit(solution)/shard_map/convert.1
  47.7 4.6 fusion.86
  52.2 7.0 %bitcast_add_fusion = f32[32,256,256]{2,1,0:T(8,128)S(1)} fusion(f32[32,256,256]{2,1,0:T(8,128)} %fusion.93, f32[32,256,256]{1,2,0:T(8,128)} %fusion.86, bf16[32,128,256]{2,1,0:T(8,128)(2,1)S(1)} %bitcast.254, bf16[32,3,256,128]{3,2,0,1:T(8,128)(2,1)S(1)} %bitcast.202), kind=kOutput, calls=%fused_computation.2 | convolution fusion | flops 541065216 | bytes 29360128 | tf_op jit(solution)/shard_map/bij,bjc->bic/dot_general | solution.py:63
  59.3 3.1 fusion.128
  63.7 3.4 fusion.150
  73.5 3.0 fusion.8
  76.5 4.5 fusion.148
  83.8 4.6 fusion.75
  88.4 10.6 %bitcast_add_fusion.2 = f32[32,256,256]{2,1,0:T(8,128)} fusion(f32[32,256,256]{2,1,0:T(8,128)} %fusion.82, f32[32,256,256]{1,2,0:T(8,128)} %fusion.75, bf16[32,128,256]{2,1,0:T(8,128)(2,1)S(1)} %bitcast.255, bf16[32,3,256,128]{3,2,0,1:T(8,128)(2,1)S(1)} %bitcast.190), kind=kOutput, calls=%fused_computation.4 | convolution fusion | flops 541065216 | bytes 29360128 | tf_op jit(solution)/shard_map/bij,bjc->bic/dot_general | solution.py:63
  99.0 6.2 %fusion.127 = (f32[32,128,256]{2,1,0:T(8,128)}, f32[32,128,256]{2,1,0:T(8,128)S(1)}) fusion(f32[32,256,256]{2,1,0:T(8,128)} %bitcast_add_fusion.2), kind=kLoop, calls=%fused_computation.195 | loop fusion | bytes 16777216 | tf_op jit(solution)/shard_map/slice | solution.py:69
  105.2 4.6 fusion.152
  113.4 16.2 %fusion.16 = bf16[32,128,256]{2,1,0:T(8,128)(2,1)} fusion(f32[32,128,1]{2,1,0:T(8,128)} %bitcast.275, f32[32,128,255]{2,1,0:T(8,128)} %bitcast.243, f32[32,128,255]{2,1,0:T(8,128)} %bitcast.242, f32[32,128,1]{2,1,0:T(8,128)} %bitcast.274, f32[32,128,1]{2,1,0:T(8,128)} %bitcast.261, f32[32,128,255]{2,1,0:T(8,128)} %bitcast.229, ...), kind=kLoop, calls=%fused_computation.33 | loop fusion | flops 23068672 | bytes 35672320 | tf_op jit(solution)/shard_map/convert_element_type | solution.py:103
  129.6 6.3 %fusion.90 = f32[32,256,256]{1,2,0:T(8,128)} fusion(bf16[32,128,256]{2,1,0:T(8,128)(2,1)} %fusion.16, bf16[32,3,256,128]{3,2,0,1:T(8,128)(2,1)S(1)} %bitcast.203), kind=kOutput, calls=%fused_computation.142 | convolution fusion | flops 536870912 | bytes 12582912 | tf_op jit(solution)/shard_map/bij,bjc->bic/dot_general | solution.py:63
  135.9 10.6 %fusion.6 = bf16[4096,256]{1,0:T(8,128)(2,1)} fusion(f32[4096,1]{1,0:T(8,128)} %get-tuple-element.67, f32[4096,255]{1,0:T(8,128)} %get-tuple-element.69, f32[4096,255]{1,0:T(8,128)} %get-tuple-element.68, f32[4096,1]{1,0:T(8,128)} %get-tuple-element.66, f32[4096,1]{1,0:T(8,128)} %get-tuple-element.59, f32[4096,255]{1,0:T(8,128)S(1)} %copy-done.18, ...), kind=kLoop, calls=%fused_computation.20 | loop fusion | flops 17825792 | bytes 27283712 | tf_op jit(solution)/shard_map/convert_element_type | solution.py:103
  147.4 4.5 collective-permute-start.2
  153.6 6.2 %fusion.79 = f32[32,256,256]{1,2,0:T(8,128)} fusion(bf16[32,128,256]{2,1,0:T(8,128)(2,1)} %fusion.16, bf16[32,3,256,128]{3,2,0,1:T(8,128)(2,1)S(1)} %bitcast.191), kind=kOutput, calls=%fused_computation.131 | convolution fusion | flops 536870912 | bytes 12582912 | tf_op jit(solution)/shard_map/bij,bjc->bic/dot_general | solution.py:63
  161.4 5.4 %fusion.87 = f32[32,256,256]{1,2,0:T(8,128)} fusion(bf16[32,128,256]{2,1,0:T(8,128)(2,1)S(1)} %bitcast.282, bf16[32,3,256,128]{3,2,0,1:T(8,128)(2,1)S(1)} %bitcast.204), kind=kOutput, calls=%fused_computation.139 | convolution fusion | flops 536870912 | bytes 12582912 | tf_op jit(solution)/shard_map/bij,bjc->bic/dot_general | solution.py:63
  167.6 8.6 %add_bitcast_fusion.4 = f32[32,256,256]{2,1,0:T(8,128)} fusion(f32[32,256,256]{1,2,0:T(8,128)} %fusion.87, f32[32,256,256]{1,2,0:T(8,128)S(1)} %bitcast.249, bf16[32,128,256]{2,1,0:T(8,128)(2,1)} %bitcast.256, bf16[32,3,256,128]{3,2,0,1:T(8,128)(2,1)S(1)} %bitcast.205), kind=kOutput, calls=%fused_computation.10 | convolution fusion | flops 541065216 | bytes 29360128 | tf_op jit(solution)/shard_map/bij,bjc->bic/dot_general | solution.py:63
  176.2 6.3 %fusion.126 = (f32[32,128,256]{2,1,0:T(8,128)}, f32[32,128,256]{2,1,0:T(8,128)S(1)}) fusion(f32[32,256,256]{2,1,0:T(8,128)} %add_bitcast_fusion.4), kind=kLoop, calls=%fused_computation.194 | loop fusion | bytes 16777216 | tf_op jit(solution)/shard_map/slice | solution.py:69
  182.4 3.4 fusion.144
  191.0 3.7 fusion.29
  194.7 4.6 fusion.142
  201.9 4.6 fusion.76
  206.5 10.3 %add_bitcast_fusion.5 = f32[32,256,256]{2,1,0:T(8,128)} fusion(f32[32,256,256]{1,2,0:T(8,128)} %fusion.76, f32[32,256,256]{1,2,0:T(8,128)} %fusion.79, bf16[32,128,256]{2,1,0:T(8,128)(2,1)S(1)} %bitcast.257, bf16[32,3,256,128]{3,2,0,1:T(8,128)(2,1)S(1)} %bitcast.193), kind=kOutput, calls=%fused_computation.11 | convolution fusion | flops 541065216 | bytes 29360128 | tf_op jit(solution)/shard_map/bij,bjc->bic/dot_general | solution.py:63
  216.8 6.2 %fusion.125 = (f32[32,128,256]{2,1,0:T(8,128)}, f32[32,128,256]{2,1,0:T(8,128)S(1)}) fusion(f32[32,256,256]{2,1,0:T(8,128)} %add_bitcast_fusion.5), kind=kLoop, calls=%fused_computation.193 | loop fusion | bytes 16777216 | tf_op jit(solution)/shard_map/slice | solution.py:69
  223.0 4.6 fusion.146
  231.3 16.2 %fusion.37 = bf16[32,128,256]{2,1,0:T(8,128)(2,1)} fusion(f32[32,128,1]{2,1,0:T(8,128)} %bitcast.273, f32[32,128,255]{2,1,0:T(8,128)} %bitcast.241, f32[32,128,255]{2,1,0:T(8,128)} %bitcast.240, f32[32,128,1]{2,1,0:T(8,128)} %bitcast.272, f32[32,128,1]{2,1,0:T(8,128)} %bitcast.263, f32[32,128,255]{2,1,0:T(8,128)} %bitcast.231, ...), kind=kLoop, calls=%fused_computation.60 | loop fusion | flops 23068672 | bytes 35672320 | tf_op jit(solution)/shard_map/convert_element_type | solution.py:103
  247.4 6.3 %fusion.91 = f32[32,256,256]{1,2,0:T(8,128)} fusion(bf16[32,128,256]{2,1,0:T(8,128)(2,1)} %fusion.37, bf16[32,3,256,128]{3,2,0,1:T(8,128)(2,1)S(1)} %bitcast.206), kind=kOutput, calls=%fused_computation.143 | convolution fusion | flops 536870912 | bytes 12582912 | tf_op jit(solution)/shard_map/bij,bjc->bic/dot_general | solution.py:63
  253.7 11.0 %fusion.27 = bf16[4096,256]{1,0:T(8,128)(2,1)} fusion(f32[4096,1]{1,0:T(8,128)} %get-tuple-element.55, f32[4096,255]{1,0:T(8,128)} %get-tuple-element.57, f32[4096,255]{1,0:T(8,128)} %get-tuple-element.56, f32[4096,1]{1,0:T(8,128)} %get-tuple-element.54, f32[4096,1]{1,0:T(8,128)} %get-tuple-element.47, f32[4096,255]{1,0:T(8,128)S(1)} %copy-done.13, ...), kind=kLoop, calls=%fused_computation.47 | loop fusion | flops 17825792 | bytes 27283712 | tf_op jit(solution)/shard_map/convert_element_type | solution.py:103
  265.7 4.5 collective-permute-start.4
  271.7 6.2 %fusion.80 = f32[32,256,256]{1,2,0:T(8,128)} fusion(bf16[32,128,256]{2,1,0:T(8,128)(2,1)} %fusion.37, bf16[32,3,256,128]{3,2,0,1:T(8,128)(2,1)S(1)} %bitcast.194), kind=kOutput, calls=%fused_computation.132 | convolution fusion | flops 536870912 | bytes 12582912 | tf_op jit(solution)/shard_map/bij,bjc->bic/dot_general | solution.py:63
  279.4 5.4 %fusion.88 = f32[32,256,256]{1,2,0:T(8,128)} fusion(bf16[32,128,256]{2,1,0:T(8,128)(2,1)S(1)} %bitcast.284, bf16[32,3,256,128]{3,2,0,1:T(8,128)(2,1)S(1)} %bitcast.207), kind=kOutput, calls=%fused_computation.140 | convolution fusion | flops 536870912 | bytes 12582912 | tf_op jit(solution)/shard_map/bij,bjc->bic/dot_general | solution.py:63
  285.6 8.6 %add_bitcast_fusion.2 = f32[32,256,256]{2,1,0:T(8,128)} fusion(f32[32,256,256]{1,2,0:T(8,128)} %fusion.88, f32[32,256,256]{1,2,0:T(8,128)S(1)} %bitcast.247, bf16[32,128,256]{2,1,0:T(8,128)(2,1)} %bitcast.258, bf16[32,3,256,128]{3,2,0,1:T(8,128)(2,1)S(1)} %bitcast.208), kind=kOutput, calls=%fused_computation.8 | convolution fusion | flops 541065216 | bytes 29360128 | tf_op jit(solution)/shard_map/bij,bjc->bic/dot_general | solution.py:63
  294.2 6.3 %fusion.124 = (f32[32,128,256]{2,1,0:T(8,128)}, f32[32,128,256]{2,1,0:T(8,128)S(1)}) fusion(f32[32,256,256]{2,1,0:T(8,128)} %add_bitcast_fusion.2), kind=kLoop, calls=%fused_computation.192 | loop fusion | bytes 16777216 | tf_op jit(solution)/shard_map/slice | solution.py:69
  300.5 3.4 fusion.138
  309.0 3.9 fusion.50
  312.9 4.6 fusion.136
  320.1 4.6 fusion.77
  324.7 10.3 %add_bitcast_fusion.3 = f32[32,256,256]{2,1,0:T(8,128)} fusion(f32[32,256,256]{1,2,0:T(8,128)} %fusion.77, f32[32,256,256]{1,2,0:T(8,128)} %fusion.80, bf16[32,128,256]{2,1,0:T(8,128)(2,1)S(1)} %bitcast.259, bf16[32,3,256,128]{3,2,0,1:T(8,128)(2,1)S(1)} %bitcast.196), kind=kOutput, calls=%fused_computation.9 | convolution fusion | flops 541065216 | bytes 29360128 | tf_op jit(solution)/shard_map/bij,bjc->bic/dot_general | solution.py:63
  335.0 6.2 %fusion.123 = (f32[32,128,256]{2,1,0:T(8,128)}, f32[32,128,256]{2,1,0:T(8,128)S(1)}) fusion(f32[32,256,256]{2,1,0:T(8,128)} %add_bitcast_fusion.3), kind=kLoop, calls=%fused_computation.191 | loop fusion | bytes 16777216 | tf_op jit(solution)/shard_map/slice | solution.py:69
  341.2 4.7 fusion.140
  349.5 16.2 %fusion.58 = bf16[32,128,256]{2,1,0:T(8,128)(2,1)} fusion(f32[32,128,1]{2,1,0:T(8,128)} %bitcast.277, f32[32,128,255]{2,1,0:T(8,128)} %bitcast.245, f32[32,128,255]{2,1,0:T(8,128)} %bitcast.244, f32[32,128,1]{2,1,0:T(8,128)} %bitcast.276, f32[32,128,1]{2,1,0:T(8,128)} %bitcast.267, f32[32,128,255]{2,1,0:T(8,128)} %bitcast.235, ...), kind=kLoop, calls=%fused_computation.87 | loop fusion | flops 23068672 | bytes 35672320 | tf_op jit(solution)/shard_map/convert_element_type | solution.py:103
  365.7 6.3 %fusion.92 = f32[32,256,256]{1,2,0:T(8,128)} fusion(bf16[32,128,256]{2,1,0:T(8,128)(2,1)} %fusion.58, bf16[32,3,256,128]{3,2,0,1:T(8,128)(2,1)S(1)} %bitcast.209), kind=kOutput, calls=%fused_computation.144 | convolution fusion | flops 536870912 | bytes 12582912 | tf_op jit(solution)/shard_map/bij,bjc->bic/dot_general | solution.py:63
  372.1 10.8 %fusion.48 = bf16[4096,256]{1,0:T(8,128)(2,1)} fusion(f32[4096,1]{1,0:T(8,128)} %get-tuple-element.43, f32[4096,255]{1,0:T(8,128)} %get-tuple-element.45, f32[4096,255]{1,0:T(8,128)} %get-tuple-element.44, f32[4096,1]{1,0:T(8,128)} %get-tuple-element.42, f32[4096,1]{1,0:T(8,128)} %get-tuple-element.35, f32[4096,255]{1,0:T(8,128)S(1)} %copy-done.20, ...), kind=kLoop, calls=%fused_computation.74 | loop fusion | flops 17825792 | bytes 27283712 | tf_op jit(solution)/shard_map/convert_element_type | solution.py:103
  383.8 4.6 collective-permute-start.6
  396.2 4.6 fusion.89
  400.8 10.9 %add_bitcast_fusion = f32[32,256,256]{2,1,0:T(8,128)} fusion(f32[32,256,256]{1,2,0:T(8,128)} %fusion.89, f32[32,256,256]{1,2,0:T(8,128)} %fusion.92, bf16[32,128,256]{2,1,0:T(8,128)(2,1)} %bitcast.252, bf16[32,3,256,128]{3,2,0,1:T(8,128)(2,1)S(1)} %bitcast.211), kind=kOutput, calls=%fused_computation.6 | convolution fusion | flops 541065216 | bytes 29360128 | tf_op jit(solution)/shard_map/bij,bjc->bic/dot_general | solution.py:63
  411.7 6.2 %fusion.122 = (f32[32,128,256]{2,1,0:T(8,128)}, f32[32,128,256]{2,1,0:T(8,128)S(1)}) fusion(f32[32,256,256]{2,1,0:T(8,128)} %add_bitcast_fusion), kind=kLoop, calls=%fused_computation.190 | loop fusion | bytes 16777216 | tf_op jit(solution)/shard_map/slice | solution.py:69
  417.9 4.6 fusion.132
  426.0 4.0 fusion.71
  430.0 4.7 fusion.130
  437.3 4.6 fusion.78
  441.9 8.0 %add_bitcast_fusion.1 = f32[32,256,256]{2,1,0:T(8,128)} fusion(f32[32,256,256]{1,2,0:T(8,128)} %fusion.78, f32[32,256,256]{1,2,0:T(8,128)S(1)} %fusion.81, bf16[32,128,256]{2,1,0:T(8,128)(2,1)S(1)} %bitcast.253, bf16[32,3,256,128]{3,2,0,1:T(8,128)(2,1)S(1)} %bitcast.199), kind=kOutput, calls=%fused_computation.7 | convolution fusion | flops 541065216 | bytes 29360128 | tf_op jit(solution)/shard_map/bij,bjc->bic/dot_general | solution.py:63
  449.9 4.0 fusion.121
  453.9 3.4 fusion.134
  462.3 7.7 %fusion.69 = bf16[4096,256]{1,0:T(8,128)(2,1)S(1)} fusion(f32[4096,1]{1,0:T(8,128)} %get-tuple-element.31, f32[4096,255]{1,0:T(8,128)} %get-tuple-element.33, f32[4096,255]{1,0:T(8,128)S(1)} %get-tuple-element.32, f32[4096,1]{1,0:T(8,128)} %get-tuple-element.30, f32[4096,1]{1,0:T(8,128)} %get-tuple-element.23, f32[4096,255]{1,0:T(8,128)S(1)} %copy-done.42, ...), kind=kLoop, calls=%fused_computation.101 | loop fusion | flops 17825792 | bytes 27283712 | tf_op jit(solution)/shard_map/convert_element_type | solution.py:103
  472.3 3.7 all-to-all-start
  478.1 2.9 all-to-all-done
  483.6 40.9 %all_to_all.10 = f32[64,256,32]{1,2,0:T(8,128)S(1)} all-to-all(f32[64,256,32]{1,2,0:T(8,128)S(1)} %copy.27), channel_id=1, replica_groups=mesh['freq'=64,'depth'=2] {'freq'}, dimensions={0} | all-to-all | bytes 4194304 | tf_op jit(solution)/shard_map/all_to_all | solution.py:42
  (190 shorter events, 90.3 us)
Async XLA Ops:
  0.0 32.8 %copy-start = (f32[256]{0:T(256)S(1)}, f32[256]{0:T(256)}, u32[]{:S(2)}) copy-start(f32[256]{0:T(256)} %param.12) | copy-start | bytes 3076
  0.9 46.4 %collective-permute-start = (bf16[128,256]{1,0:T(8,128)(2,1)S(1)}, bf16[128,256]{1,0:T(8,128)(2,1)S(1)}, u32[]{:S(2)}, u32[]{:S(2)}) collective-permute-start(bf16[128,256]{1,0:T(8,128)(2,1)S(1)} %get-tuple-element.85), channel_id=1, source_target_pairs={{0,1},{2,3},{4,5},{6,7},{8,9},{10,11},{12,13},{14,15},{16,17},{18,... | collective-permute-start | bytes 196616 | tf_op jit(solution)/shard_map/ppermute | solution.py:20
  4.8 42.5 %collective-permute-start.1 = (bf16[128,256]{1,0:T(8,128)(2,1)S(1)}, bf16[128,256]{1,0:T(8,128)(2,1)S(1)}, u32[]{:S(2)}, u32[]{:S(2)}) collective-permute-start(bf16[128,256]{1,0:T(8,128)(2,1)S(1)} %get-tuple-element.84), channel_id=1, source_target_pairs={{1,0},{3,2},{5,4},{7,6},{9,8},{11,10},{13,12},{15,14},{17,16},{19,... | collective-permute-start | bytes 196616 | tf_op jit(solution)/shard_map/ppermute | solution.py:22
  16.0 7.0 %copy-start.3 = (bf16[32,128,3,2,128]{4,1,3,0,2:T(8,128)(2,1)}, bf16[32,128,3,2,128]{4,1,3,0,2:T(8,128)(2,1)S(1)}, u32[]{:S(2)}) copy-start(bf16[32,128,3,2,128]{4,1,3,0,2:T(8,128)(2,1)S(1)} %copy.23) | copy-start | bytes 18874372
  16.0 7.0 %copy-start.21 = (bf16[4096,256]{1,0:T(8,128)(2,1)S(1)}, bf16[4096,256]{1,0:T(8,128)(2,1)}, u32[]{:S(2)}) copy-start(bf16[4096,256]{1,0:T(8,128)(2,1)} %param.9) | copy-start | bytes 6291460
  23.0 5.2 copy-start.2
  28.2 11.9 %copy-start.56 = (s32[512]{0:T(512)S(1)}, s32[512]{0:T(512)}, u32[]{:S(2)}) copy-start(s32[512]{0:T(512)} %param.14) | copy-start | bytes 6148
  40.6 7.0 %copy-start.4 = (bf16[32,128,3,2,128]{4,1,3,0,2:T(8,128)(2,1)S(1)}, bf16[32,128,3,2,128]{4,1,3,0,2:T(8,128)(2,1)}, u32[]{:S(2)}) copy-start(bf16[32,128,3,2,128]{4,1,3,0,2:T(8,128)(2,1)} %copy-done.3) | copy-start | bytes 18874372
  47.6 4.6 copy-start.35
  47.6 4.6 copy-start.23
  59.3 4.5 copy-start.5
  67.1 5.1 copy-start.8
  67.1 6.4 %copy-start.43 = (f32[32,128,256]{2,1,0:T(8,128)S(1)}, f32[32,128,256]{2,1,0:T(8,128)}, u32[]{:S(2)}) copy-start(f32[32,128,256]{2,1,0:T(8,128)} %get-tuple-element.20) | copy-start | bytes 12582916
  67.8 3.4 copy-start.28
  73.5 10.3 %slice-start = ((s8[6291456]{0:T(1024)(128)(4,1)}), s8[4194304]{0:T(1024)(128)(4,1)S(1)}, s32[]{:S(2)}) async-start(s8[6291456]{0:T(1024)(128)(4,1)} %bitcast.187), calls=%async_computation.2 | async-start | bytes 8388608
  76.5 7.2 %slice-start.1 = ((s8[6291456]{0:T(1024)(128)(4,1)}), s8[2097152]{0:T(1024)(128)(4,1)S(1)}, s32[]{:S(2)}) async-start(s8[6291456]{0:T(1024)(128)(4,1)} %bitcast.187), calls=%async_computation.3 | async-start | bytes 4194304
  81.1 2.7 copy-start.36
  83.8 4.6 copy-start.24
  109.8 3.7 copy-start.7
  129.6 6.3 %copy-start.17 = (f32[4096,255]{1,0:T(8,128)S(1)}, f32[4096,255]{1,0:T(8,128)}, u32[]{:S(2)}) copy-start(f32[4096,255]{1,0:T(8,128)} %get-tuple-element.60) | copy-start | bytes 12533764
  129.6 6.3 %copy-start.18 = (f32[4096,255]{1,0:T(8,128)S(1)}, f32[4096,255]{1,0:T(8,128)}, u32[]{:S(2)}) copy-start(f32[4096,255]{1,0:T(8,128)} %get-tuple-element.61) | copy-start | bytes 12533764
  147.4 12.3 %collective-permute-start.2 = (bf16[128,256]{1,0:T(8,128)(2,1)S(1)}, bf16[128,256]{1,0:T(8,128)(2,1)S(1)}, u32[]{:S(2)}, u32[]{:S(2)}) collective-permute-start(bf16[128,256]{1,0:T(8,128)(2,1)S(1)} %get-tuple-element.81), channel_id=1, source_target_pairs={{0,1},{2,3},{4,5},{6,7},{8,9},{10,11},{12,13},{14,15},{16,17},{18,... | collective-permute-start | bytes 196616 | tf_op jit(solution)/shard_map/ppermute | solution.py:20
  152.0 7.8 %copy-start.46 = (bf16[4096,256]{1,0:T(8,128)(2,1)S(1)}, bf16[4096,256]{1,0:T(8,128)(2,1)}, u32[]{:S(2)}) copy-start(bf16[4096,256]{1,0:T(8,128)(2,1)} %fusion.6) | copy-start | bytes 6291460
  152.0 7.8 %collective-permute-start.3 = (bf16[128,256]{1,0:T(8,128)(2,1)S(1)}, bf16[128,256]{1,0:T(8,128)(2,1)S(1)}, u32[]{:S(2)}, u32[]{:S(2)}) collective-permute-start(bf16[128,256]{1,0:T(8,128)(2,1)S(1)} %get-tuple-element.80), channel_id=1, source_target_pairs={{1,0},{3,2},{5,4},{7,6},{9,8},{11,10},{13,12},{15,14},{17,16},{19,... | collective-permute-start | bytes 196616 | tf_op jit(solution)/shard_map/ppermute | solution.py:22
  159.8 7.0 %slice-start.4 = ((s8[8388608]{0:T(1024)(128)(4,1)}), s8[4194304]{0:T(1024)(128)(4,1)S(1)}, s32[]{:S(2)}) async-start(s8[8388608]{0:T(1024)(128)(4,1)} %bitcast.248), calls=%async_computation.6 | async-start | bytes 8388608
  161.4 5.4 %copy-start.37 = (bf16[4096,256]{1,0:T(8,128)(2,1)}, bf16[4096,256]{1,0:T(8,128)(2,1)S(1)}, u32[]{:S(2)}) copy-start(bf16[4096,256]{1,0:T(8,128)(2,1)S(1)} %get-tuple-element.79) | copy-start | bytes 6291460
  161.4 6.2 %slice-start.5 = ((s8[8388608]{0:T(1024)(128)(4,1)}), s8[4194304]{0:T(1024)(128)(4,1)S(1)}, s32[]{:S(2)}) async-start(s8[8388608]{0:T(1024)(128)(4,1)} %bitcast.248), calls=%async_computation.7 | async-start | bytes 8388608
  185.9 5.1 copy-start.11
  186.6 3.4 copy-start.30
  201.9 4.6 copy-start.25
  227.6 3.7 copy-start.10
  227.6 3.7 copy-start.55
  247.4 6.3 %copy-start.12 = (f32[4096,255]{1,0:T(8,128)S(1)}, f32[4096,255]{1,0:T(8,128)}, u32[]{:S(2)}) copy-start(f32[4096,255]{1,0:T(8,128)} %get-tuple-element.48) | copy-start | bytes 12533764
  247.4 6.3 %copy-start.13 = (f32[4096,255]{1,0:T(8,128)S(1)}, f32[4096,255]{1,0:T(8,128)}, u32[]{:S(2)}) copy-start(f32[4096,255]{1,0:T(8,128)} %get-tuple-element.49) | copy-start | bytes 12533764
  247.4 6.3 %copy-start.54 = (f32[4096]{0:T(1024)S(1)}, f32[4096]{0:T(1024)}, u32[]{:S(2)}) copy-start(f32[4096]{0:T(1024)} %get-tuple-element.98) | copy-start | bytes 49156
  265.7 12.2 %collective-permute-start.4 = (bf16[128,256]{1,0:T(8,128)(2,1)S(1)}, bf16[128,256]{1,0:T(8,128)(2,1)S(1)}, u32[]{:S(2)}, u32[]{:S(2)}) collective-permute-start(bf16[128,256]{1,0:T(8,128)(2,1)S(1)} %get-tuple-element.77), channel_id=1, source_target_pairs={{0,1},{2,3},{4,5},{6,7},{8,9},{10,11},{12,13},{14,15},{16,17},{18,... | collective-permute-start | bytes 196616 | tf_op jit(solution)/shard_map/ppermute | solution.py:20
  270.2 7.6 %copy-start.47 = (bf16[4096,256]{1,0:T(8,128)(2,1)S(1)}, bf16[4096,256]{1,0:T(8,128)(2,1)}, u32[]{:S(2)}) copy-start(bf16[4096,256]{1,0:T(8,128)(2,1)} %fusion.27) | copy-start | bytes 6291460
  270.2 7.6 %collective-permute-start.5 = (bf16[128,256]{1,0:T(8,128)(2,1)S(1)}, bf16[128,256]{1,0:T(8,128)(2,1)S(1)}, u32[]{:S(2)}, u32[]{:S(2)}) collective-permute-start(bf16[128,256]{1,0:T(8,128)(2,1)S(1)} %get-tuple-element.76), channel_id=1, source_target_pairs={{1,0},{3,2},{5,4},{7,6},{9,8},{11,10},{13,12},{15,14},{17,16},{19,... | collective-permute-start | bytes 196616 | tf_op jit(solution)/shard_map/ppermute | solution.py:22
  277.8 7.0 %slice-start.2 = ((s8[8388608]{0:T(1024)(128)(4,1)}), s8[4194304]{0:T(1024)(128)(4,1)S(1)}, s32[]{:S(2)}) async-start(s8[8388608]{0:T(1024)(128)(4,1)} %bitcast.246), calls=%async_computation.4 | async-start | bytes 8388608
  279.4 5.4 %copy-start.39 = (bf16[4096,256]{1,0:T(8,128)(2,1)}, bf16[4096,256]{1,0:T(8,128)(2,1)S(1)}, u32[]{:S(2)}) copy-start(bf16[4096,256]{1,0:T(8,128)(2,1)S(1)} %get-tuple-element.75) | copy-start | bytes 6291460
  279.4 6.2 %slice-start.3 = ((s8[8388608]{0:T(1024)(128)(4,1)}), s8[4194304]{0:T(1024)(128)(4,1)S(1)}, s32[]{:S(2)}) async-start(s8[8388608]{0:T(1024)(128)(4,1)} %bitcast.246), calls=%async_computation.5 | async-start | bytes 8388608
  303.9 5.1 copy-start.16
  304.6 3.4 copy-start.32
  320.1 4.6 copy-start.26
  345.9 3.7 copy-start.15
  345.9 3.7 copy-start.53
  365.7 6.3 %copy-start.19 = (f32[4096,255]{1,0:T(8,128)S(1)}, f32[4096,255]{1,0:T(8,128)}, u32[]{:S(2)}) copy-start(f32[4096,255]{1,0:T(8,128)} %get-tuple-element.36) | copy-start | bytes 12533764
  365.7 6.3 %copy-start.20 = (f32[4096,255]{1,0:T(8,128)S(1)}, f32[4096,255]{1,0:T(8,128)}, u32[]{:S(2)}) copy-start(f32[4096,255]{1,0:T(8,128)} %get-tuple-element.37) | copy-start | bytes 12533764
  365.7 6.3 %copy-start.52 = (f32[4096]{0:T(1024)S(1)}, f32[4096]{0:T(1024)}, u32[]{:S(2)}) copy-start(f32[4096]{0:T(1024)} %get-tuple-element.97) | copy-start | bytes 49156
  383.8 8.8 %collective-permute-start.6 = (bf16[128,256]{1,0:T(8,128)(2,1)S(1)}, bf16[128,256]{1,0:T(8,128)(2,1)S(1)}, u32[]{:S(2)}, u32[]{:S(2)}) collective-permute-start(bf16[128,256]{1,0:T(8,128)(2,1)S(1)} %get-tuple-element.73), channel_id=1, source_target_pairs={{0,1},{2,3},{4,5},{6,7},{8,9},{10,11},{12,13},{14,15},{16,17},{18,... | collective-permute-start | bytes 196616 | tf_op jit(solution)/shard_map/ppermute | solution.py:20
  388.3 6.3 %copy-start.48 = (bf16[4096,256]{1,0:T(8,128)(2,1)S(1)}, bf16[4096,256]{1,0:T(8,128)(2,1)}, u32[]{:S(2)}) copy-start(bf16[4096,256]{1,0:T(8,128)(2,1)} %fusion.48) | copy-start | bytes 6291460
  388.3 6.3 %collective-permute-start.7 = (bf16[128,256]{1,0:T(8,128)(2,1)S(1)}, bf16[128,256]{1,0:T(8,128)(2,1)S(1)}, u32[]{:S(2)}, u32[]{:S(2)}) collective-permute-start(bf16[128,256]{1,0:T(8,128)(2,1)S(1)} %get-tuple-element.72), channel_id=1, source_target_pairs={{1,0},{3,2},{5,4},{7,6},{9,8},{11,10},{13,12},{15,14},{17,16},{19,... | collective-permute-start | bytes 196616 | tf_op jit(solution)/shard_map/ppermute | solution.py:22
  396.2 4.6 copy-start.33
  422.5 3.5 copy-start.45
  434.6 2.7 copy-start.34
  437.3 4.6 copy-start.22
  457.3 3.7 copy-start.41
  457.3 5.0 copy-start.42
  457.3 5.0 copy-start.51
  462.2 7.7 %copy-start.57 = (s32[512]{0:T(512)S(1)}, s32[512]{0:T(512)}, u32[]{:S(2)}) copy-start(s32[512]{0:T(512)} %broadcast_subtract_fusion) | copy-start | bytes 6148
  470.0 6.0 %copy-start.49 = (bf16[128,1,2048]{2,0,1:T(8,128)(2,1)S(1)}, bf16[128,1,2048]{2,0,1:T(8,128)(2,1)}, u32[]{:S(2)}) copy-start(bf16[128,1,2048]{2,0,1:T(8,128)(2,1)} %get-tuple-element.90) | copy-start | bytes 1572868
  470.0 6.0 %copy-start.50 = (bf16[128,1,2048]{2,0,1:T(8,128)(2,1)S(1)}, bf16[128,1,2048]{2,0,1:T(8,128)(2,1)}, u32[]{:S(2)}) copy-start(bf16[128,1,2048]{2,0,1:T(8,128)(2,1)} %get-tuple-element.91) | copy-start | bytes 1572868
  472.3 8.8 %all-to-all-start = ((bf16[2,256,256]{2,1,0:T(8,128)(2,1)}), bf16[2,256,256]{2,1,0:T(8,128)(2,1)S(1)}, u32[]{:S(2)}, u32[]{:S(2)}) async-start(bf16[2,256,256]{2,1,0:T(8,128)(2,1)} %bitcast.89), calls=%async_computation | async-start | bytes 524288 | tf_op jit(solution)/shard_map/all_to_all | solution.py:36
  482.4 42.9 %copy-start.1 = (f32[256]{0:T(256)S(1)}, f32[256]{0:T(256)}, u32[]{:S(2)}) copy-start(f32[256]{0:T(256)} %param.12) | copy-start | bytes 3076
  (9 other events, 21.2 us)
where the time goes:
time: 532 us; the launch traced here: 526 us
  local copies, waits for them, and re-layouts  170 us (32%)
  matrix products  160 us (30%)
  other arithmetic  122 us (23%)
  blocking collectives  40.9 us (8%)
  starting transfers between devices  27 us (5%)
    dot_general x24, matrix products, apply_blocks(): jnp.einsum('bij,bjc->bic', ordered[:, offset], stacked[offset:offset + bl...  156 us
    convert_element_type x7, other arithmetic, local(): columns = (damping[:, None] * combined).astype(jnp.bfloat16)  88.7 us
    slice x24, local copies, waits for them, and re-layouts, times_unit(): lower = jnp.roll(values, 1, axis=1)  74.9 us
    slice x8, local copies, waits for them, and re-layouts, apply_blocks(): real_part = product[:, :block_size].reshape(block_count * block_size, width)  44.5 us
    all_to_all x1, blocking collectives, summed_on_arrival_2(): lax.all_to_all(parts, axis, split_axis=0, concat_axis=0, tiled=True)  40.9 us
    unnamed x128, local copies, waits for them, and re-layouts  25.3 us
    ppermute x4, starting transfers between devices, padded_2(): lax.ppermute(tail, axis, [(i, (i + 1) % count) for i in range(ends)])  17.6 us
    add x4, other arithmetic, apply_blocks(): return real_part + times_unit(imag_part)  14.6 us
  transfers between devices with their start and end apart: 9, of which 2 were waited for; matrix products, arithmetic and copies ran while one was open for 11% of the time, Pallas kernels for 0%

commit v1 on v0

v1 whole, which is shorter than its diff:
```python
import math

import jax
import jax.numpy as jnp
from jax import lax
from jax.experimental import pallas as pl
from jax.experimental.pallas import tpu as pltpu
from jax.sharding import Mesh, PartitionSpec as P

NT = 2048
STEPS = 4
BS = 128
F32 = jnp.float32
BF16 = jnp.bfloat16
CHUNKS = 8
UNROLL = 8

VMEM_SPEC = pl.BlockSpec(memory_space=pltpu.VMEM)
HBM_SPEC = pl.BlockSpec(memory_space=pl.ANY)
SMEM_SPEC = pl.BlockSpec(memory_space=pltpu.SMEM)


def limit(mebibytes):
    return pltpu.CompilerParams(vmem_limit_bytes=mebibytes << 20)


def in_hbm(x):
    return pltpu.with_memory_space_constraint(x, pltpu.HBM)


def vmem(shape, dtype):
    return pltpu.VMEM(shape, dtype)


def split_matrix(width):
    half = width // 2
    source = lax.broadcasted_iota(jnp.int32, (width, width), 0)
    target = lax.broadcasted_iota(jnp.int32, (width, width), 1)
    return jnp.where(source == 2 * (target % half) + target // half, 1.0, 0.0).astype(F32)


def put_block(ref, b, field):
    half = field.shape[1] // 2
    at = b * (2 * BS)
    if not isinstance(at, int):
        at = pl.multiple_of(at, 2 * BS)
    real = field[:, :half]
    imag = field[:, half:]
    ref[pl.ds(at, BS), :] = field
    ref[pl.ds(at + BS, BS), :half] = -imag
    ref[pl.ds(at + BS, BS), half:] = real


def advanced(ordered, stacked, weights, first_row, floor_row):
    product = jnp.dot(ordered, stacked, preferred_element_type=F32)
    size = product.shape[0] // 2
    half = product.shape[1] // 2
    wr = weights[0:1, :half]
    wi = weights[0:1, half:]
    side_real = product[size:, :half]
    side_imag = product[size:, half:]
    real = product[:size, :half] + (wr * side_real - wi * side_imag)
    imag = product[:size, half:] + (wr * side_imag + wi * side_real)
    row = first_row + lax.broadcasted_iota(jnp.int32, (size, half), 0)
    damping = jnp.where(row >= floor_row, 0.5, 1.0).astype(F32)
    return jnp.concatenate([damping * real, damping * imag], axis=1).astype(BF16)


def zero_ends(ref):
    edge = jnp.zeros((2 * BS, ref.shape[1]), ref.dtype)
    ref[0 : 2 * BS, :] = edge
    ref[ref.shape[0] - 2 * BS :, :] = edge


def first_step(
    main_hbm, side_hbm, field_hbm, coupling_hbm, floors_hbm,
    ordered_ref, start_ref, next_ref, weight_ref,
    main_buf, side_buf, field_buf, planes, coupling_buf, floors_buf, sems, small_sems,
):
    blocks = ordered_ref.shape[0]
    per = blocks // CHUNKS
    rows = per * BS
    op_rows = rows * 6
    width = field_buf.shape[1]
    coupling_copy = pltpu.make_async_copy(coupling_hbm, coupling_buf, small_sems.at[0])
    floors_copy = pltpu.make_async_copy(floors_hbm, floors_buf, small_sems.at[1])
    coupling_copy.start()
    floors_copy.start()
    copies = []
    for n in range(CHUNKS):
        copies.append(
            [
                pltpu.make_async_copy(
                    source.at[pl.ds(n * size, size), :], buf.at[pl.ds(n * size, size), :], sems.at[kind, n]
                )
                for kind, (source, buf, size) in enumerate(
                    ((field_hbm, field_buf, rows), (main_hbm, main_buf, op_rows), (side_hbm, side_buf, op_rows))
                )
            ]
        )
    copies[0][0].start()
    copies[1][0].start()
    for n in range(CHUNKS):
        copies[n][1].start()
        copies[n][2].start()
        if n + 2 < CHUNKS:
            copies[n + 2][0].start()
    perm = split_matrix(width)
    for ref in (start_ref, next_ref):
        zero_ends(ref)
    coupling_copy.wait()
    floors_copy.wait()
    weights = jnp.dot(
        jnp.broadcast_to(coupling_buf[...], (8, width)), perm, preferred_element_type=F32, precision=lax.Precision.HIGHEST
    )
    weight_ref[...] = weights
    perm = perm.astype(BF16)
    first_row = lax.axis_index("depth") * (blocks * BS)
    floor_row = floors_buf[0] - first_row

    def split_chunk(n):
        copies[n][0].wait()
        for j in range(per):
            b = n * per + j
            field = jnp.dot(field_buf[b * BS : (b + 1) * BS, :], perm, preferred_element_type=F32).astype(BF16)
            put_block(start_ref, b + 1, field)

    split_chunk(0)
    for n in range(CHUNKS):
        if n + 1 < CHUNKS:
            split_chunk(n + 1)
        copies[n][1].wait()
        copies[n][2].wait()
        for j in range(per):
            b = n * per + j
            for kind, buf in enumerate((main_buf, side_buf)):
                plane = planes.at[j * 2 + kind]
                plane[...] = buf[b * BS * 6 : (b + 1) * BS * 6, :].astype(F32)
                for m in range(6):
                    ordered_ref[b, kind * BS : (kind + 1) * BS, m * BS : (m + 1) * BS] = plane[
                        pl.ds(m, BS, stride=6), :
                    ].astype(BF16)
        for j in range(per):
            b = n * per + j
            stacked = start_ref[b * 2 * BS : (b + 3) * 2 * BS, :]
            put_block(next_ref, b + 1, advanced(ordered_ref[b], stacked, weights, b * BS, floor_row))


def whole_step(step, last):
    def kernel(ordered_ref, field_ref, weight_ref, floors_ref, next_ref):
        blocks = ordered_ref.shape[0]
        first_row = lax.axis_index("depth") * (blocks * BS)
        floor_row = floors_ref[step] - first_row
        weights = weight_ref[...]
        if last:
            next_ref[blocks * BS :, :] = jnp.zeros((next_ref.shape[0] - blocks * BS, next_ref.shape[1]), F32)
        else:
            zero_ends(next_ref)

        def some(n, carry):
            for j in range(UNROLL):
                b = n * UNROLL + j
                at = pl.multiple_of(b * BS, BS)
                stacked = field_ref[pl.ds(pl.multiple_of(at * 2, 2 * BS), 6 * BS), :]
                field = advanced(ordered_ref[b], stacked, weights, at, floor_row)
                if last:
                    next_ref[pl.ds(at, BS), :] = field.astype(F32)
                else:
                    put_block(next_ref, b + 1, field)
            return carry

        lax.fori_loop(0, blocks // UNROLL, some, 0)

    return kernel


def edge_block(step, ordered_ref, field_ref, weight_ref, floors_ref, halo_ref, halo_buf):
    blocks = ordered_ref.shape[0]
    side = lax.axis_index("depth")
    halo = halo_ref[...]
    if step == 0:
        halo = jnp.dot(halo, split_matrix(halo.shape[1]).astype(BF16), preferred_element_type=F32).astype(BF16)
    b = (blocks - 1) * (1 - side)
    size = 2 * BS
    at = pl.multiple_of(b * size, size)
    halo_buf[size : 2 * size, :] = field_ref[pl.ds(at + size, size), :]
    inner = pl.multiple_of(at + 2 * size * side, size)
    halo_buf[pl.ds(pl.multiple_of(2 * size * side, size), size), :] = field_ref[pl.ds(inner, size), :]
    put_block(halo_buf, 2 * (1 - side), halo)
    first_row = side * (blocks * BS)
    field = advanced(ordered_ref[b], halo_buf[...], weight_ref[...], b * BS, floors_ref[step] - first_row)
    return b, field


def edge_step(step):
    def kernel(ordered_ref, field_ref, weight_ref, floors_ref, halo_ref, in_ref, next_ref, out_ref, halo_buf):
        del in_ref
        b, field = edge_block(step, ordered_ref, field_ref, weight_ref, floors_ref, halo_ref, halo_buf)
        out_ref[...] = field
        put_block(next_ref, b + 1, field)

    return kernel


def edge_and_pick(
    ordered_ref, field_ref, weight_ref, floors_ref, halo_ref, in_ref, receivers_ref,
    final_ref, keep_ref, send_ref, halo_buf, picked,
):
    del in_ref
    b, field = edge_block(STEPS - 1, ordered_ref, field_ref, weight_ref, floors_ref, halo_ref, halo_buf)
    final_ref[pl.ds(pl.multiple_of(b * BS, BS), BS), :] = field.astype(F32)
    rows = ordered_ref.shape[0] * BS
    side = lax.axis_index("depth")
    owned = keep_ref.shape[0]
    group = 8
    for out_ref, owner in ((send_ref, 1 - side), (keep_ref, side)):

        def some(n, carry):
            for j in range(group):
                local = receivers_ref[owner * owned + n * group + j] - side * rows
                inside = jnp.logical_and(local >= 0, local < rows)
                at = jnp.where(inside, local, rows)
                picked[pl.ds(n * group + j, 1), :] = final_ref[pl.ds(at, 1), :]
            return carry

        lax.fori_loop(0, owned // group, some, 0)
        out_ref[...] = picked[...].astype(BF16)


def basis_kernel(freq_ref, out_ref):
    core = lax.axis_index("core")
    spread = 32
    lanes = freq_ref.shape[1]
    chip = (lax.axis_index("x") * lax.axis_size("y") + lax.axis_index("y")) * lax.axis_size("zh") + lax.axis_index("zh")
    turn = 2.0 * math.pi

    def unit(count_times_freq):
        cycles = count_times_freq * (1.0 / NT)
        angle = turn * (cycles - jnp.floor(cycles))
        return jnp.cos(angle), jnp.sin(angle)

    sample = (core * spread + lax.broadcasted_iota(jnp.int32, (spread, lanes), 0)).astype(F32)
    state = []
    turns = []
    for which in (core, 1 - core):
        freq = jnp.broadcast_to(freq_ref[pl.ds(chip * 2 + which, 1), :], (spread, lanes))
        state += list(unit(freq * sample))
        turns.append(unit(freq * (2.0 * spread)))

    def some(q, state):
        at = pl.multiple_of(q * spread, spread)
        out = []
        for which in range(2):
            c, s = state[2 * which], state[2 * which + 1]
            tc, ts = turns[which]
            out_ref[pl.ds(at, spread), 2 * which * lanes : (2 * which + 1) * lanes] = c.astype(BF16)
            out_ref[pl.ds(at, spread), (2 * which + 1) * lanes : (2 * which + 2) * lanes] = (-s).astype(BF16)
            out += [c * tc - s * ts, s * tc + c * ts]
        return tuple(out)

    lax.fori_loop(0, NT // (2 * spread), some, tuple(state))


def series_kernel(basis_ref, keep_ref, got_ref, keep2_ref, got2_ref, out_ref):
    picked = jnp.concatenate([keep_ref[...] + got_ref[...], keep2_ref[...] + got2_ref[...]], axis=1)
    product = lax.dot_general(basis_ref[...], picked, (((1,), (1,)), ((), ())), preferred_element_type=F32)
    out_ref[...] = product.astype(BF16)


def local(pressure_field, block_main, block_coupled, coupling, frequencies, receivers, floors):
    rows, width = pressure_field.shape
    blocks = rows // BS
    side = lax.axis_index("depth")
    swap = [(0, 1), (1, 0)]
    halo = lax.ppermute(lax.dynamic_slice_in_dim(pressure_field, (1 - side) * (rows - BS), BS, 0), "depth", swap)

    padded = ((blocks + 2) * 2 * BS, width)
    halo_buf = pltpu.VMEM((6 * BS, width), BF16)
    ordered, start, field, weights = pl.pallas_call(
        first_step,
        out_shape=(
            vmem((blocks, 2 * BS, 6 * BS), BF16),
            vmem(padded, BF16),
            vmem(padded, BF16),
            vmem((8, width), F32),
        ),
        in_specs=[HBM_SPEC] * 5,
        out_specs=(VMEM_SPEC,) * 4,
        scratch_shapes=[
            pltpu.VMEM((rows * 6, BS), BF16),
            pltpu.VMEM((rows * 6, BS), BF16),
            pltpu.VMEM((rows, width), BF16),
            pltpu.VMEM((2 * blocks // CHUNKS, BS * 6, BS), F32),
            pltpu.VMEM((1, width), F32),
            pltpu.SMEM((STEPS,), jnp.int32),
            pltpu.SemaphoreType.DMA((3, CHUNKS)),
            pltpu.SemaphoreType.DMA((2,)),
        ],
        compiler_params=limit(28),
        name="first_step",
    )(
        in_hbm(block_main.reshape(rows * 6, BS)),
        in_hbm(block_coupled.reshape(rows * 6, BS)),
        in_hbm(pressure_field),
        in_hbm(coupling.reshape(1, width)),
        in_hbm(floors),
    )

    before = start
    for step in range(STEPS - 1):
        field, edge = pl.pallas_call(
            edge_step(step),
            out_shape=(vmem(padded, BF16), vmem((BS, width), BF16)),
            in_specs=[VMEM_SPEC] * 3 + [SMEM_SPEC] + [VMEM_SPEC] * 2,
            out_specs=(VMEM_SPEC,) * 2,
            input_output_aliases={5: 0},
            scratch_shapes=[halo_buf],
            compiler_params=limit(6),
            name="edge_step",
        )(ordered, before, weights, floors, halo, field)
        halo = lax.ppermute(edge, "depth", swap)
        last = step == STEPS - 2
        before = field
        field = pl.pallas_call(
            whole_step(step + 1, last),
            out_shape=vmem((rows + 8, width), F32) if last else vmem(padded, BF16),
            in_specs=[VMEM_SPEC] * 3 + [SMEM_SPEC],
            out_specs=VMEM_SPEC,
            compiler_params=limit(6),
            name="whole_step",
        )(ordered, before, weights, floors)

    owned = receivers.shape[0] // lax.axis_size("depth")
    _, keep, send = pl.pallas_call(
        edge_and_pick,
        out_shape=(vmem((rows + 8, width), F32), vmem((owned, width), BF16), vmem((owned, width), BF16)),
        in_specs=[VMEM_SPEC] * 3 + [SMEM_SPEC] + [VMEM_SPEC] * 2 + [SMEM_SPEC],
        out_specs=(VMEM_SPEC,) * 3,
        input_output_aliases={5: 0},
        scratch_shapes=[halo_buf, pltpu.VMEM((owned, width), F32)],
        compiler_params=limit(6),
        name="edge_and_pick",
    )(ordered, before, weights, floors, halo, field, receivers)

    got = lax.ppermute(send, "depth", swap)
    keep2 = lax.ppermute(keep, "core", swap)
    basis = pl.pallas_call(
        basis_kernel,
        out_shape=vmem((NT // 2, 2 * width), BF16),
        in_specs=[VMEM_SPEC],
        out_specs=VMEM_SPEC,
        compiler_params=limit(8),
        name="basis",
    )(frequencies.reshape(-1, width // 2))
    got2 = lax.ppermute(got, "core", swap)
    partial = pl.pallas_call(
        series_kernel,
        out_shape=jax.ShapeDtypeStruct((NT // 2, owned), BF16),
        in_specs=[VMEM_SPEC] * 5,
        out_specs=VMEM_SPEC,
        compiler_params=limit(8),
        name="series",
    )(basis, keep, got, keep2, got2)
    others = ("x", "y", "zh")
    groups = lax.axis_size(others)
    arrived = lax.all_to_all(
        partial.reshape(groups, NT // 2 // groups, owned), others, split_axis=0, concat_axis=0, tiled=True
    )
    summed = arrived.astype(F32).sum(axis=0) * (1.0 / math.sqrt(frequencies.shape[0]))
    return summed.T


def solution(mesh):
    chips = Mesh(mesh.devices.reshape(4, 4, 2, 2, 2), ("x", "y", "zh", "core", "depth"))
    freq = ("x", "y", "zh", "core")
    in_specs = (
        P("depth", freq),
        P("depth", None, None, None),
        P("depth", None, None, None),
        P(freq),
        P(),
        P(),
        P(),
    )
    return jax.shard_map(local, mesh=chips, in_specs=in_specs, out_specs=P("depth", freq), check_vma=False)
```

time: 532 us -> 73.6 us (0.14); the launches traced: 526 us -> 73.4 us
  local copies, waits for them, and re-layouts: 170 us -> 0.86 us
  matrix products: 160 us -> 0 us
  other arithmetic: 122 us -> 0.7 us
  Pallas kernels: 0 us -> 36.9 us
  starting transfers between devices: 27 us -> 6.57 us
  blocking collectives: 40.9 us -> 24.4 us
    dot_general x26 -> x0, matrix products: 160 us -> none  [the longest x24 156 us: apply_blocks(): jnp.einsum('bij,bjc->bic', ordered[:, offset], stacked[offset:offset + bl...]
    slice x37 -> x0, local copies, waits for them, and re-layouts: 124 us -> none  [the longest x24 74.9 us: times_unit(): lower = jnp.roll(values, 1, axis=1)]
    convert_element_type x7 -> x0, other arithmetic: 88.7 us -> none  [local(): columns = (damping[:, None] * combined).astype(jnp.bfloat16)]
    pallas_call x0 -> x10, Pallas kernels: none -> 36.9 us  [the longest x1 15 us: local(): pl.pallas_call(first_step, out_shape=(vmem((blocks, 2 * BS, 6 * BS), BF16...]
    unnamed x128 -> x6, local copies, waits for them, and re-layouts: 25.3 us -> 0.01 us
    ppermute x8 -> x7, starting transfers between devices: 23.3 us -> 6.57 us  [the longest x3 2.46 us: local(): halo = lax.ppermute(edge, 'depth', swap)]
    all_to_all x1, blocking collectives: 40.9 us -> 24.4 us  [local(): lax.all_to_all(partial.reshape(groups, NT // 2 // groups, owned), others,...]
    add x4 -> x0, other arithmetic: 14.6 us -> none  [apply_blocks(): return real_part + times_unit(imag_part)]
  transfers between devices with their start and end apart: 9 -> 7, of which waited for: 2 -> 2; matrix products, arithmetic and copies ran while one was open for 11% -> 0% of each run, Pallas kernels for 0% -> 41%
where the time goes in v1:
time: 73.6 us; the launch traced here: 73.4 us
  Pallas kernels  36.9 us (50%)
  blocking collectives  24.4 us (33%)
  starting transfers between devices  6.57 us (9%)
  waiting for transfers between devices  3.77 us (5%)
  local copies, waits for them, and re-layouts  0.86 us (1%)
    all_to_all x1, blocking collectives, local(): lax.all_to_all(partial.reshape(groups, NT // 2 // groups, owned), others,...  24.4 us
    pallas_call x1, Pallas kernels, local(): pl.pallas_call(first_step, out_shape=(vmem((blocks, 2 * BS, 6 * BS), BF16...  15 us
    pallas_call x3, Pallas kernels, local(): pl.pallas_call(whole_step(step + 1, last), out_shape=vmem((rows + 8, widt...  14.6 us
    pallas_call x1, Pallas kernels, local(): pl.pallas_call(edge_and_pick, out_shape=(vmem((rows + 8, width), F32), vm...  3.58 us
    ppermute x1, waiting for transfers between devices, local(): got = lax.ppermute(send, 'depth', swap)  2.97 us
    pallas_call x3, Pallas kernels, local(): pl.pallas_call(edge_step(step), out_shape=(vmem(padded, BF16), vmem((BS,...  2.7 us
    ppermute x3, starting transfers between devices, local(): halo = lax.ppermute(edge, 'depth', swap)  2.46 us
    ppermute x1, starting transfers between devices, local(): got = lax.ppermute(send, 'depth', swap)  2.08 us
  transfers between devices with their start and end apart: 7, of which 2 were waited for; matrix products, arithmetic and copies ran while one was open for 0% of the time, Pallas kernels for 41%

profile of v1, /device:TPU:0, one launch (start us, length us, event | category | flops | bytes accessed | tf_op | source)
XLA Modules:
  0.0 73.4 jit_solution(1418343307882369414)
XLA Ops:
  0.0 0.8 %constant_dynamic-slice_fusion = bf16[128,256]{1,0:T(8,128)(2,1)S(1)} fusion(bf16[4096,256]{1,0:T(8,128)(2,1)} %field_hbm.1, s32[]{:T(128)S(6)} %select_n.3), kind=kLoop, calls=%fused_computation.2 | loop fusion | bytes 131076 | tf_op jit(solution)/shard_map/dynamic_slice | solution.py:275
  0.8 2.0 %collective-permute-start = (bf16[128,256]{1,0:T(8,128)(2,1)S(1)}, bf16[128,256]{1,0:T(8,128)(2,1)S(1)}, u32[]{:S(2)}, u32[]{:S(2)}) collective-permute-start(bf16[128,256]{1,0:T(8,128)(2,1)S(1)} %constant_dynamic-slice_fusion), channel_id=1, source_target_pairs={{0,1},{1,0},{2,3},{3,2},{4,5},{5,4},{6,7},{7,6},{8,9},{9,8},{10,11... | collective-permute-start | bytes 196616 | tf_op jit(solution)/shard_map/ppermute | solution.py:275
  2.9 0.0 copy-start
  2.9 15.0 %first_step.1 = (bf16[32,256,768]{2,1,0:T(8,128)(2,1)S(1)}, bf16[8704,256]{1,0:T(8,128)(2,1)S(1)}, bf16[8704,256]{1,0:T(8,128)(2,1)S(1)}, f32[8,256]{1,0:T(8,128)S(1)}) custom-call(bf16[24576,128]{1,0:T(8,128)(2,1)} %bitcast.9, bf16[24576,128]{1,0:T(8,128)(2,1)} %bitcast.10, bf16[4096,256]{1,0:T(8,128)(2,1)} %field_hbm.1, f32[1,256]{1,0:T(1,128)} %bitcast.11, ...), custom_call_target="tpu_custom_call" | custom-call | tf_op jit(solution)/shard_map/first_step/pallas_call | solution.py:279
  17.9 0.0 collective-permute-done.halo_ref
  17.9 0.0 copy-done
  17.9 1.0 %edge_step.3 = (bf16[8704,256]{1,0:T(8,128)(2,1)S(1)}, bf16[128,256]{1,0:T(8,128)(2,1)S(1)}) custom-call(bf16[32,256,768]{2,1,0:T(8,128)(2,1)S(1)} %get-tuple-element.17.ordered_ref, bf16[8704,256]{1,0:T(8,128)(2,1)S(1)} %get-tuple-element.18.field_ref, f32[8,256]{1,0:T(8,128)S(1)} %get-tuple-element.19.weight_ref, ...), custom_call_target="tpu_custom_call", output_to_operand_aliasing={{0}: (5, {})} | custom-call | tf_op jit(solution)/shard_map/edge_step/pallas_call | solution.py:311
  18.9 0.1 collective-permute-start.1
  19.0 4.9 %whole_step.3.in_ref = bf16[8704,256]{1,0:T(8,128)(2,1)S(1)} custom-call(bf16[32,256,768]{2,1,0:T(8,128)(2,1)S(1)} %get-tuple-element.17.ordered_ref, bf16[8704,256]{1,0:T(8,128)(2,1)S(1)} %get-tuple-element.21.field_ref, f32[8,256]{1,0:T(8,128)S(1)} %get-tuple-element.19.weight_ref, s32[4]{0:T(128)S(1)} %copy-done), custom_call_target="tpu_custom_call" | custom-call | tf_op jit(solution)/shard_map/whole_step/pallas_call | solution.py:324
  23.9 0.0 collective-permute-done.1.halo_ref
  23.9 0.9 %edge_step.4 = (bf16[8704,256]{1,0:T(8,128)(2,1)S(1)}, bf16[128,256]{1,0:T(8,128)(2,1)S(1)}) custom-call(bf16[32,256,768]{2,1,0:T(8,128)(2,1)S(1)} %get-tuple-element.17.ordered_ref, bf16[8704,256]{1,0:T(8,128)(2,1)S(1)} %get-tuple-element.21.field_ref, f32[8,256]{1,0:T(8,128)S(1)} %get-tuple-element.19.weight_ref, ...), custom_call_target="tpu_custom_call", output_to_operand_aliasing={{0}: (5, {})} | custom-call | tf_op jit(solution)/shard_map/edge_step/pallas_call | solution.py:311
  24.8 2.1 %collective-permute-start.2 = (bf16[128,256]{1,0:T(8,128)(2,1)S(1)}, bf16[128,256]{1,0:T(8,128)(2,1)S(1)}, u32[]{:S(2)}, u32[]{:S(2)}) collective-permute-start(bf16[128,256]{1,0:T(8,128)(2,1)S(1)} %get-tuple-element.24), channel_id=1, source_target_pairs={{0,1},{1,0},{2,3},{3,2},{4,5},{5,4},{6,7},{7,6},{8,9},{9,8},{10,11... | collective-permute-start | bytes 196616 | tf_op jit(solution)/shard_map/ppermute | solution.py:321
  26.9 5.0 %whole_step.4.in_ref = bf16[8704,256]{1,0:T(8,128)(2,1)S(1)} custom-call(bf16[32,256,768]{2,1,0:T(8,128)(2,1)S(1)} %get-tuple-element.17.ordered_ref, bf16[8704,256]{1,0:T(8,128)(2,1)S(1)} %get-tuple-element.23.field_ref, f32[8,256]{1,0:T(8,128)S(1)} %get-tuple-element.19.weight_ref, s32[4]{0:T(128)S(1)} %copy-done), custom_call_target="tpu_custom_call" | custom-call | tf_op jit(solution)/shard_map/whole_step/pallas_call | solution.py:324
  31.9 0.0 collective-permute-done.2.halo_ref
  31.9 0.9 %edge_step.5 = (bf16[8704,256]{1,0:T(8,128)(2,1)S(1)}, bf16[128,256]{1,0:T(8,128)(2,1)S(1)}) custom-call(bf16[32,256,768]{2,1,0:T(8,128)(2,1)S(1)} %get-tuple-element.17.ordered_ref, bf16[8704,256]{1,0:T(8,128)(2,1)S(1)} %get-tuple-element.23.field_ref, f32[8,256]{1,0:T(8,128)S(1)} %get-tuple-element.19.weight_ref, ...), custom_call_target="tpu_custom_call", output_to_operand_aliasing={{0}: (5, {})} | custom-call | tf_op jit(solution)/shard_map/edge_step/pallas_call | solution.py:311
  32.7 0.3 collective-permute-start.3
  33.0 0.0 copy-start.2
  33.0 4.8 %whole_step.5.in_ref = f32[4104,256]{1,0:T(8,128)S(1)} custom-call(bf16[32,256,768]{2,1,0:T(8,128)(2,1)S(1)} %get-tuple-element.17.ordered_ref, bf16[8704,256]{1,0:T(8,128)(2,1)S(1)} %get-tuple-element.25.field_ref, f32[8,256]{1,0:T(8,128)S(1)} %get-tuple-element.19.weight_ref, s32[4]{0:T(128)S(1)} %copy-done), custom_call_target="tpu_custom_call" | custom-call | tf_op jit(solution)/shard_map/whole_step/pallas_call | solution.py:324
  37.8 0.0 copy-start.1
  37.8 0.0 collective-permute-done.3.halo_ref
  37.8 0.0 copy-done.2
  37.8 3.6 %edge_and_pick.1 = (f32[4104,256]{1,0:T(8,128)S(1)}, bf16[256,256]{1,0:T(8,128)(2,1)S(1)}, bf16[256,256]{1,0:T(8,128)(2,1)S(1)}) custom-call(bf16[32,256,768]{2,1,0:T(8,128)(2,1)S(1)} %get-tuple-element.17.ordered_ref, bf16[8704,256]{1,0:T(8,128)(2,1)S(1)} %get-tuple-element.25.field_ref, ...), custom_call_target="tpu_custom_call", output_to_operand_aliasing={{0}: (5, {})} | custom-call | tf_op jit(solution)/shard_map/edge_and_pick/pallas_call | solution.py:334
  41.4 2.1 %collective-permute-start.4 = (bf16[256,256]{1,0:T(8,128)(2,1)S(1)}, bf16[256,256]{1,0:T(8,128)(2,1)S(1)}, u32[]{:S(2)}, u32[]{:S(2)}) collective-permute-start(bf16[256,256]{1,0:T(8,128)(2,1)S(1)} %get-tuple-element.28), channel_id=1, source_target_pairs={{0,1},{1,0},{2,3},{3,2},{4,5},{5,4},{6,7},{7,6},{8,9},{9,8},{10,11... | collective-permute-start | bytes 393224 | tf_op jit(solution)/shard_map/ppermute | solution.py:345
  43.5 0.0 collective-permute-start.5
  43.5 3.0 %collective-permute-done.4.got_ref = bf16[256,256]{1,0:T(8,128)(2,1)S(1)} collective-permute-done((bf16[256,256]{1,0:T(8,128)(2,1)S(1)}, bf16[256,256]{1,0:T(8,128)(2,1)S(1)}, u32[]{:S(2)}, u32[]{:S(2)}) %collective-permute-start.4) | collective-permute-done | bytes 131104 | tf_op jit(solution)/shard_map/ppermute | solution.py:345
  46.5 0.0 collective-permute-start.6
  46.5 0.0 copy-done.1
  46.5 0.5 basis.1.basis_ref
  47.0 0.0 collective-permute-done.5.keep2_ref
  47.0 0.8 %collective-permute-done.6.got2_ref = bf16[256,256]{1,0:T(8,128)(2,1)S(1)} collective-permute-done((bf16[256,256]{1,0:T(8,128)(2,1)S(1)}, bf16[256,256]{1,0:T(8,128)(2,1)S(1)}, u32[]{:S(2)}, u32[]{:S(2)}) %collective-permute-start.6) | collective-permute-done | bytes 131104 | tf_op jit(solution)/shard_map/ppermute | solution.py:355
  47.8 0.5 series.1
  48.3 24.4 %all_to_all.5 = bf16[32,32,256]{2,1,0:T(8,128)(2,1)S(1)} all-to-all(bf16[32,32,256]{2,1,0:T(8,128)(2,1)S(1)} %bitcast.7), channel_id=1, replica_groups=mesh['x'=4,'y'=4,'zh'=2,'core'=2,'depth'=2] {'x','y','zh'}, dimensions={0} | all-to-all | bytes 1048576 | tf_op jit(solution)/shard_map/all_to_all | solution.py:366
  72.7 0.1 convert_reduce_fusion
  72.8 0.6 multiply_bitcast_fusion
Async XLA Ops:
  0.8 17.1 %collective-permute-start = (bf16[128,256]{1,0:T(8,128)(2,1)S(1)}, bf16[128,256]{1,0:T(8,128)(2,1)S(1)}, u32[]{:S(2)}, u32[]{:S(2)}) collective-permute-start(bf16[128,256]{1,0:T(8,128)(2,1)S(1)} %constant_dynamic-slice_fusion), channel_id=1, source_target_pairs={{0,1},{1,0},{2,3},{3,2},{4,5},{5,4},{6,7},{7,6},{8,9},{9,8},{10,11... | collective-permute-start | bytes 196616 | tf_op jit(solution)/shard_map/ppermute | solution.py:275
  2.9 15.1 %copy-start = (s32[4]{0:T(128)S(1)}, s32[4]{0:T(128)}, u32[]{:S(2)}) copy-start(s32[4]{0:T(128)} %floors_ref.13) | copy-start | bytes 52
  18.9 5.0 %collective-permute-start.1 = (bf16[128,256]{1,0:T(8,128)(2,1)S(1)}, bf16[128,256]{1,0:T(8,128)(2,1)S(1)}, u32[]{:S(2)}, u32[]{:S(2)}) collective-permute-start(bf16[128,256]{1,0:T(8,128)(2,1)S(1)} %get-tuple-element.22), channel_id=1, source_target_pairs={{0,1},{1,0},{2,3},{3,2},{4,5},{5,4},{6,7},{7,6},{8,9},{9,8},{10,11... | collective-permute-start | bytes 196616 | tf_op jit(solution)/shard_map/ppermute | solution.py:321
  24.8 7.1 %collective-permute-start.2 = (bf16[128,256]{1,0:T(8,128)(2,1)S(1)}, bf16[128,256]{1,0:T(8,128)(2,1)S(1)}, u32[]{:S(2)}, u32[]{:S(2)}) collective-permute-start(bf16[128,256]{1,0:T(8,128)(2,1)S(1)} %get-tuple-element.24), channel_id=1, source_target_pairs={{0,1},{1,0},{2,3},{3,2},{4,5},{5,4},{6,7},{7,6},{8,9},{9,8},{10,11... | collective-permute-start | bytes 196616 | tf_op jit(solution)/shard_map/ppermute | solution.py:321
  32.7 5.1 %collective-permute-start.3 = (bf16[128,256]{1,0:T(8,128)(2,1)S(1)}, bf16[128,256]{1,0:T(8,128)(2,1)S(1)}, u32[]{:S(2)}, u32[]{:S(2)}) collective-permute-start(bf16[128,256]{1,0:T(8,128)(2,1)S(1)} %get-tuple-element.26), channel_id=1, source_target_pairs={{0,1},{1,0},{2,3},{3,2},{4,5},{5,4},{6,7},{7,6},{8,9},{9,8},{10,11... | collective-permute-start | bytes 196616 | tf_op jit(solution)/shard_map/ppermute | solution.py:321
  33.0 4.8 %copy-start.2 = (s32[512]{0:T(512)S(1)}, s32[512]{0:T(512)}, u32[]{:S(2)}) copy-start(s32[512]{0:T(512)} %receivers_ref.1) | copy-start | bytes 6148
  37.8 8.7 %copy-start.1 = (f32[8192]{0:T(1024)S(1)}, f32[8192]{0:T(1024)}, u32[]{:S(2)}) copy-start(f32[8192]{0:T(1024)} %param.11) | copy-start | bytes 98308
  41.4 5.0 %collective-permute-start.4 = (bf16[256,256]{1,0:T(8,128)(2,1)S(1)}, bf16[256,256]{1,0:T(8,128)(2,1)S(1)}, u32[]{:S(2)}, u32[]{:S(2)}) collective-permute-start(bf16[256,256]{1,0:T(8,128)(2,1)S(1)} %get-tuple-element.28), channel_id=1, source_target_pairs={{0,1},{1,0},{2,3},{3,2},{4,5},{5,4},{6,7},{7,6},{8,9},{9,8},{10,11... | collective-permute-start | bytes 393224 | tf_op jit(solution)/shard_map/ppermute | solution.py:345
  43.5 3.5 %collective-permute-start.5 = (bf16[256,256]{1,0:T(8,128)(2,1)S(1)}, bf16[256,256]{1,0:T(8,128)(2,1)S(1)}, u32[]{:S(2)}, u32[]{:S(2)}) collective-permute-start(bf16[256,256]{1,0:T(8,128)(2,1)S(1)} %get-tuple-element.27.keep_ref), channel_id=1, source_target_pairs={{0,2},{2,0},{1,3},{3,1},{4,6},{6,4},{5,7},{7,5},{8,10},{10,8},{9,1... | collective-permute-start | bytes 393224 | tf_op jit(solution)/shard_map/ppermute | solution.py:346
  46.5 1.3 %collective-permute-start.6 = (bf16[256,256]{1,0:T(8,128)(2,1)S(1)}, bf16[256,256]{1,0:T(8,128)(2,1)S(1)}, u32[]{:S(2)}, u32[]{:S(2)}) collective-permute-start(bf16[256,256]{1,0:T(8,128)(2,1)S(1)} %collective-permute-done.4.got_ref), channel_id=1, source_target_pairs={{0,2},{2,0},{1,3},{3,1},{4,6},{6,4},{5,7},{7,5},{8,10},{10,8},{9,1... | collective-permute-start | bytes 393224 | tf_op jit(solution)/shard_map/ppermute | solution.py:355

commit v2 on v1

v2 whole, which is shorter than its diff:
```python
import math

import jax
import jax.numpy as jnp
from jax import lax
from jax.experimental import pallas as pl
from jax.experimental.pallas import tpu as pltpu
from jax.sharding import Mesh, PartitionSpec as P

NT = 2048
STEPS = 4
BS = 128
F32 = jnp.float32
BF16 = jnp.bfloat16
CHUNKS = 8
AHEAD = 2
UNROLL = 8

VMEM_SPEC = pl.BlockSpec(memory_space=pltpu.VMEM)
HBM_SPEC = pl.BlockSpec(memory_space=pl.ANY)


def limit(mebibytes):
    return pltpu.CompilerParams(vmem_limit_bytes=mebibytes << 20)


def in_hbm(x):
    return pltpu.with_memory_space_constraint(x, pltpu.HBM)


def vmem(shape, dtype):
    return pltpu.VMEM(shape, dtype)


def split_matrix(width):
    half = width // 2
    source = lax.broadcasted_iota(jnp.int32, (width, width), 0)
    target = lax.broadcasted_iota(jnp.int32, (width, width), 1)
    return jnp.where(source == 2 * (target % half) + target // half, 1.0, 0.0).astype(F32)


def put_block(ref, b, field):
    half = field.shape[1] // 2
    at = b * (2 * BS)
    if not isinstance(at, int):
        at = pl.multiple_of(at, 2 * BS)
    real = field[:, :half]
    imag = field[:, half:]
    ref[0, pl.ds(at, BS), :] = real
    ref[1, pl.ds(at, BS), :] = imag
    ref[0, pl.ds(at + BS, BS), :] = -imag
    ref[1, pl.ds(at + BS, BS), :] = real


def three_blocks(ref, b):
    at = b * (2 * BS)
    if not isinstance(at, int):
        at = pl.multiple_of(at, 2 * BS)
    return jnp.concatenate([ref[0, pl.ds(at, 6 * BS), :], ref[1, pl.ds(at, 6 * BS), :]], axis=1)


def operator_rows(ordered_ref, b):
    return jnp.concatenate([ordered_ref[b, m] for m in range(ordered_ref.shape[1])], axis=1)


def advanced(ordered, stacked, weights, first_row, floor_rows):
    product = jnp.dot(ordered, stacked, preferred_element_type=F32)
    size = product.shape[0] // 2
    half = product.shape[1] // 2
    wr = weights[0:1, :half]
    wi = weights[0:1, half:]
    side_real = product[size:, :half]
    side_imag = product[size:, half:]
    real = product[:size, :half] + (wr * side_real - wi * side_imag)
    imag = product[:size, half:] + (wr * side_imag + wi * side_real)
    row = first_row + lax.broadcasted_iota(jnp.int32, (size, half), 0)
    damping = jnp.where(row >= floor_rows, 0.5, 1.0).astype(F32)
    return jnp.concatenate([damping * real, damping * imag], axis=1).astype(BF16)


def put_final(ref, at, field):
    half = field.shape[1] // 2
    ref[0, pl.ds(at, BS), :] = field[:, :half].astype(F32)
    ref[1, pl.ds(at, BS), :] = field[:, half:].astype(F32)


def zero_ends(ref):
    edge = jnp.zeros((2, 2 * BS, ref.shape[2]), ref.dtype)
    ref[:, 0 : 2 * BS, :] = edge
    ref[:, ref.shape[1] - 2 * BS :, :] = edge


def first_step(
    main_hbm, side_hbm, field_hbm, coupling_hbm, floors_hbm,
    receivers_hbm, ordered_ref, start_ref, next_ref, weight_ref, floor_ref, pick_ref,
    main_buf, side_buf, field_buf, planes, coupling_buf, floors_buf, receivers_buf, sems, small_sems,
):
    blocks = ordered_ref.shape[0]
    per = blocks // CHUNKS
    rows = per * BS
    op_rows = rows * 6
    width = field_buf.shape[1]
    coupling_copy = pltpu.make_async_copy(coupling_hbm, coupling_buf, small_sems.at[0])
    floors_copy = pltpu.make_async_copy(floors_hbm, floors_buf, small_sems.at[1])
    receivers_copy = pltpu.make_async_copy(receivers_hbm, receivers_buf, small_sems.at[2])
    coupling_copy.start()
    floors_copy.start()
    receivers_copy.start()
    copies = []
    for n in range(CHUNKS):
        copies.append(
            [
                pltpu.make_async_copy(
                    source.at[pl.ds(n * size, size), :], buf.at[pl.ds(n * size, size), :], sems.at[kind, n]
                )
                for kind, (source, buf, size) in enumerate(
                    ((field_hbm, field_buf, rows), (main_hbm, main_buf, op_rows), (side_hbm, side_buf, op_rows))
                )
            ]
        )
    copies[0][0].start()
    for n in range(AHEAD):
        copies[n + 1][0].start()
        copies[n][1].start()
        copies[n][2].start()
    perm = split_matrix(width)
    for ref in (start_ref, next_ref):
        zero_ends(ref)
    coupling_copy.wait()
    floors_copy.wait()
    weights = jnp.dot(
        jnp.broadcast_to(coupling_buf[...], (8, width)), perm, preferred_element_type=F32, precision=lax.Precision.HIGHEST
    )
    weight_ref[...] = weights
    perm = perm.astype(BF16)
    first_row = lax.axis_index("depth") * (blocks * BS)
    lanes = floor_ref.shape
    floors = jnp.zeros(lanes, jnp.int32)
    for step in range(STEPS):
        floors = jnp.where(lax.broadcasted_iota(jnp.int32, lanes, 0) == step, floors_buf[step] - first_row, floors)
    floor_ref[...] = floors
    receivers_copy.wait()
    local = receivers_buf[...] - first_row
    pick_ref[...] = jnp.where(jnp.logical_and(local >= 0, local < blocks * BS), local, blocks * BS)

    def split_chunk(n):
        for j in range(per):
            b = n * per + j
            field = jnp.dot(field_buf[b * BS : (b + 1) * BS, :], perm, preferred_element_type=F32).astype(BF16)
            put_block(start_ref, b + 1, field)

    def order_block(n, j):
        b = n * per + j
        for kind, buf in enumerate((main_buf, side_buf)):
            plane = planes.at[(n % 2) * 2 * per + j * 2 + kind]
            plane[...] = buf[b * BS * 6 : (b + 1) * BS * 6, :].astype(F32)
            for m in range(6):
                ordered_ref[b, m, kind * BS : (kind + 1) * BS, :] = plane[pl.ds(m, BS, stride=6), :].astype(BF16)

    def march_block(b):
        field = advanced(
            operator_rows(ordered_ref, b), three_blocks(start_ref, b), weights, b * BS, floors[0:1, : width // 2]
        )
        put_block(next_ref, b + 1, field)

    always = lax.axis_index("depth") >= 0
    copies[0][0].wait()
    split_chunk(0)
    for n in range(CHUNKS + 1):
        if n < CHUNKS:
            copies[n][1].wait()
            copies[n][2].wait()
            if n + AHEAD < CHUNKS:
                copies[n + AHEAD][1].start()
                copies[n + AHEAD][2].start()
                if n + AHEAD + 1 < CHUNKS:
                    copies[n + AHEAD + 1][0].start()
            if n + 1 < CHUNKS:
                copies[n + 1][0].wait()

        @pl.when(always)
        def _(n=n):
            for j in range(per):
                if n > 0:
                    march_block((n - 1) * per + j)
                if n < CHUNKS:
                    order_block(n, j)
            if n + 1 < CHUNKS:
                split_chunk(n + 1)


def whole_step(step, last):
    def kernel(ordered_ref, field_ref, weight_ref, floor_ref, next_ref):
        blocks = ordered_ref.shape[0]
        floors = floor_ref[step : step + 1, :]
        weights = weight_ref[...]
        if last:
            next_ref[:, blocks * BS :, :] = jnp.zeros((2, next_ref.shape[1] - blocks * BS, next_ref.shape[2]), F32)
        else:
            zero_ends(next_ref)

        def some(n, carry):
            for j in range(UNROLL):
                b = n * UNROLL + j
                at = pl.multiple_of(b * BS, BS)
                field = advanced(operator_rows(ordered_ref, b), three_blocks(field_ref, b), weights, at, floors)
                if last:
                    put_final(next_ref, at, field)
                else:
                    put_block(next_ref, b + 1, field)
            return carry

        lax.fori_loop(0, blocks // UNROLL, some, 0)

    return kernel


def edge_block(step, ordered_ref, field_ref, weight_ref, floor_ref, halo_ref, halo_buf):
    blocks = ordered_ref.shape[0]
    side = lax.axis_index("depth")
    halo = halo_ref[...]
    if step == 0:
        halo = jnp.dot(halo, split_matrix(halo.shape[1]).astype(BF16), preferred_element_type=F32).astype(BF16)
    b = (blocks - 1) * (1 - side)
    size = 2 * BS
    at = pl.multiple_of(b * size, size)
    halo_buf[:, size : 2 * size, :] = field_ref[:, pl.ds(at + size, size), :]
    inner = pl.multiple_of(at + 2 * size * side, size)
    halo_buf[:, pl.ds(pl.multiple_of(2 * size * side, size), size), :] = field_ref[:, pl.ds(inner, size), :]
    put_block(halo_buf, 2 * (1 - side), halo)
    field = advanced(
        operator_rows(ordered_ref, b), three_blocks(halo_buf, 0), weight_ref[...], b * BS, floor_ref[step : step + 1, :]
    )
    return b, field


def edge_step(step):
    def kernel(ordered_ref, field_ref, weight_ref, floor_ref, halo_ref, in_ref, next_ref, out_ref, halo_buf):
        del in_ref
        b, field = edge_block(step, ordered_ref, field_ref, weight_ref, floor_ref, halo_ref, halo_buf)
        out_ref[...] = field
        put_block(next_ref, b + 1, field)

    return kernel


def edge_and_pick(
    ordered_ref, field_ref, weight_ref, floor_ref, halo_ref, in_ref, rows_vmem,
    final_ref, keep_ref, send_ref, halo_buf, picked, rows_ref, sem,
):
    del in_ref
    rows_copy = pltpu.make_async_copy(rows_vmem, rows_ref, sem)
    rows_copy.start()
    b, field = edge_block(STEPS - 1, ordered_ref, field_ref, weight_ref, floor_ref, halo_ref, halo_buf)
    put_final(final_ref, pl.multiple_of(b * BS, BS), field)
    side = lax.axis_index("depth")
    owned = keep_ref.shape[0]
    lanes = rows_ref.shape[1]
    group = 32
    rows_copy.wait()
    for out_ref, owner in ((send_ref, 1 - side), (keep_ref, side)):

        def some(n, carry):
            for j in range(group):
                at = rows_ref[owner * (owned // lanes) + n // (lanes // group), (n % (lanes // group)) * group + j]
                picked[0, pl.ds(n * group + j, 1), :] = final_ref[0, pl.ds(at, 1), :]
                picked[1, pl.ds(n * group + j, 1), :] = final_ref[1, pl.ds(at, 1), :]
            return carry

        lax.fori_loop(0, owned // group, some, 0)
        out_ref[...] = jnp.concatenate([picked[0], picked[1]], axis=1).astype(BF16)


def basis_kernel(freq_ref, out_ref):
    core = lax.axis_index("core")
    spread = 32
    lanes = freq_ref.shape[1]
    chip = (lax.axis_index("x") * lax.axis_size("y") + lax.axis_index("y")) * lax.axis_size("zh") + lax.axis_index("zh")
    turn = 2.0 * math.pi

    def unit(count_times_freq):
        cycles = count_times_freq * (1.0 / NT)
        angle = turn * (cycles - jnp.floor(cycles))
        return jnp.cos(angle), jnp.sin(angle)

    sample = (core * spread + lax.broadcasted_iota(jnp.int32, (spread, lanes), 0)).astype(F32)
    state = []
    turns = []
    for which in (core, 1 - core):
        freq = jnp.broadcast_to(freq_ref[pl.ds(chip * 2 + which, 1), :], (spread, lanes))
        state += list(unit(freq * sample))
        turns.append(unit(freq * (2.0 * spread)))

    def some(q, state):
        at = pl.multiple_of(q * spread, spread)
        out = []
        for which in range(2):
            c, s = state[2 * which], state[2 * which + 1]
            tc, ts = turns[which]
            out_ref[pl.ds(at, spread), 2 * which * lanes : (2 * which + 1) * lanes] = c.astype(BF16)
            out_ref[pl.ds(at, spread), (2 * which + 1) * lanes : (2 * which + 2) * lanes] = (-s).astype(BF16)
            out += [c * tc - s * ts, s * tc + c * ts]
        return tuple(out)

    lax.fori_loop(0, NT // (2 * spread), some, tuple(state))


def series_kernel(basis_ref, keep_ref, got_ref, keep2_ref, got2_ref, out_ref):
    picked = jnp.concatenate([keep_ref[...] + got_ref[...], keep2_ref[...] + got2_ref[...]], axis=1)
    product = lax.dot_general(basis_ref[...], picked, (((1,), (1,)), ((), ())), preferred_element_type=F32)
    out_ref[...] = product.astype(BF16)


def local(pressure_field, block_main, block_coupled, coupling, frequencies, receivers, floors):
    rows, width = pressure_field.shape
    blocks = rows // BS
    side = lax.axis_index("depth")
    swap = [(0, 1), (1, 0)]
    halo = lax.ppermute(lax.dynamic_slice_in_dim(pressure_field, (1 - side) * (rows - BS), BS, 0), "depth", swap)

    padded = (2, (blocks + 2) * 2 * BS, width // 2)
    halo_buf = pltpu.VMEM((2, 6 * BS, width // 2), BF16)
    ordered, start, field, weights, floor_rows, pick_rows = pl.pallas_call(
        first_step,
        out_shape=(
            vmem((blocks, 6, 2 * BS, BS), BF16),
            vmem(padded, BF16),
            vmem(padded, BF16),
            vmem((8, width), F32),
            vmem((8, width // 2), jnp.int32),
            vmem((receivers.shape[0] // BS, BS), jnp.int32),
        ),
        in_specs=[HBM_SPEC] * 6,
        out_specs=(VMEM_SPEC,) * 6,
        scratch_shapes=[
            pltpu.VMEM((rows * 6, BS), BF16),
            pltpu.VMEM((rows * 6, BS), BF16),
            pltpu.VMEM((rows, width), BF16),
            pltpu.VMEM((4 * blocks // CHUNKS, BS * 6, BS), F32),
            pltpu.VMEM((1, width), F32),
            pltpu.SMEM((STEPS,), jnp.int32),
            pltpu.VMEM((receivers.shape[0] // BS, BS), jnp.int32),
            pltpu.SemaphoreType.DMA((3, CHUNKS)),
            pltpu.SemaphoreType.DMA((3,)),
        ],
        compiler_params=limit(28),
        name="first_step",
    )(
        in_hbm(block_main.reshape(rows * 6, BS)),
        in_hbm(block_coupled.reshape(rows * 6, BS)),
        in_hbm(pressure_field),
        in_hbm(coupling.reshape(1, width)),
        in_hbm(floors),
        in_hbm(receivers.reshape(-1, BS)),
    )

    before = start
    for step in range(STEPS - 1):
        field, edge = pl.pallas_call(
            edge_step(step),
            out_shape=(vmem(padded, BF16), vmem((BS, width), BF16)),
            in_specs=[VMEM_SPEC] * 6,
            out_specs=(VMEM_SPEC,) * 2,
            input_output_aliases={5: 0},
            scratch_shapes=[halo_buf],
            compiler_params=limit(6),
            name="edge_step",
        )(ordered, before, weights, floor_rows, halo, field)
        halo = lax.ppermute(edge, "depth", swap)
        last = step == STEPS - 2
        before = field
        field = pl.pallas_call(
            whole_step(step + 1, last),
            out_shape=vmem((2, rows + 8, width // 2), F32) if last else vmem(padded, BF16),
            in_specs=[VMEM_SPEC] * 4,
            out_specs=VMEM_SPEC,
            compiler_params=limit(6),
            name="whole_step",
        )(ordered, before, weights, floor_rows)

    owned = receivers.shape[0] // lax.axis_size("depth")
    _, keep, send = pl.pallas_call(
        edge_and_pick,
        out_shape=(vmem((2, rows + 8, width // 2), F32), vmem((owned, width), BF16), vmem((owned, width), BF16)),
        in_specs=[VMEM_SPEC] * 7,
        out_specs=(VMEM_SPEC,) * 3,
        input_output_aliases={5: 0},
        scratch_shapes=[
            halo_buf,
            pltpu.VMEM((2, owned, width // 2), F32),
            pltpu.SMEM(pick_rows.shape, jnp.int32),
            pltpu.SemaphoreType.DMA,
        ],
        compiler_params=limit(6),
        name="edge_and_pick",
    )(ordered, before, weights, floor_rows, halo, field, pick_rows)

    got = lax.ppermute(send, "depth", swap)
    keep2 = lax.ppermute(keep, "core", swap)
    basis = pl.pallas_call(
        basis_kernel,
        out_shape=vmem((NT // 2, 2 * width), BF16),
        in_specs=[VMEM_SPEC],
        out_specs=VMEM_SPEC,
        compiler_params=limit(8),
        cost_estimate=pl.CostEstimate(flops=4_000_000_000, bytes_accessed=0, transcendentals=0),
        name="basis",
    )(frequencies.reshape(-1, width // 2))
    got2 = lax.ppermute(got, "core", swap)
    partial = pl.pallas_call(
        series_kernel,
        out_shape=jax.ShapeDtypeStruct((NT // 2, owned), BF16),
        in_specs=[VMEM_SPEC] * 5,
        out_specs=VMEM_SPEC,
        compiler_params=limit(8),
        name="series",
    )(basis, keep, got, keep2, got2)
    others = ("x", "y", "zh")
    groups = lax.axis_size(others)
    arrived = lax.all_to_all(
        partial.reshape(groups, NT // 2 // groups, owned), others, split_axis=0, concat_axis=0, tiled=True
    )
    summed = arrived.astype(F32).sum(axis=0) * (1.0 / math.sqrt(frequencies.shape[0]))
    return summed.T


def solution(mesh):
    chips = Mesh(mesh.devices.reshape(4, 4, 2, 2, 2), ("x", "y", "zh", "core", "depth"))
    freq = ("x", "y", "zh", "core")
    in_specs = (
        P("depth", freq),
        P("depth", None, None, None),
        P("depth", None, None, None),
        P(freq),
        P(),
        P(),
        P(),
    )
    return jax.shard_map(local, mesh=chips, in_specs=in_specs, out_specs=P("depth", freq), check_vma=False)
```

time: 73.6 us -> 63.8 us (0.87)
  Pallas kernels: 36.9 us -> 27.2 us
    pallas_call x5, Pallas kernels: 33.2 us -> 25 us  [the longest x3 12.9 us: local(): pl.pallas_call(whole_step(step + 1, last), out_shape=vmem((2, rows + 8, w...]
    pallas_call x3, Pallas kernels: 2.7 us -> 1.14 us  [local(): pl.pallas_call(edge_step(step), out_shape=(vmem(padded, BF16), vmem((BS,...]
  transfers between devices with their start and end apart: 7 -> 7, of which waited for: 2 -> 3; matrix products, arithmetic and copies ran while one was open for 0% -> 0% of each run, Pallas kernels for 41% -> 37%
where the time goes in v2:
time: 63.8 us; the launch traced here: 63.6 us
  Pallas kernels  27.2 us (43%)
  blocking collectives  24.3 us (38%)
  starting transfers between devices  6.47 us (10%)
  waiting for transfers between devices  4 us (6%)
  local copies, waits for them, and re-layouts  0.85 us (1%)
  other arithmetic  0.7 us (1%)
    all_to_all x1, blocking collectives, local(): lax.all_to_all(partial.reshape(groups, NT // 2 // groups, owned), others,...  24.3 us
    pallas_call x3, Pallas kernels, local(): pl.pallas_call(whole_step(step + 1, last), out_shape=vmem((2, rows + 8, w...  12.9 us
    pallas_call x1, Pallas kernels, local(): pl.pallas_call(first_step, out_shape=(vmem((blocks, 6, 2 * BS, BS), BF16)...  10.2 us
    ppermute x1, waiting for transfers between devices, local(): got = lax.ppermute(send, 'depth', swap)  3.06 us
    ppermute x3, starting transfers between devices, local(): halo = lax.ppermute(edge, 'depth', swap)  2.45 us
    ppermute x1, starting transfers between devices, local(): lax.ppermute(lax.dynamic_slice_in_dim(pressure_field, (1 - side) * (rows...  2.03 us
    ppermute x1, starting transfers between devices, local(): got = lax.ppermute(send, 'depth', swap)  1.99 us
    pallas_call x1, Pallas kernels, local(): pl.pallas_call(edge_and_pick, out_shape=(vmem((2, rows + 8, width // 2),...  1.92 us
  transfers between devices with their start and end apart: 7, of which 3 were waited for; matrix products, arithmetic and copies ran while one was open for 0% of the time, Pallas kernels for 37%

profile of v2, /device:TPU:0, one launch (start us, length us, event | category | flops | bytes accessed | tf_op | source)
XLA Modules:
  0.0 63.6 jit_solution(13487215858015667687)
XLA Ops:
  0.0 0.8 %constant_dynamic-slice_fusion = bf16[128,256]{1,0:T(8,128)(2,1)S(1)} fusion(bf16[4096,256]{1,0:T(8,128)(2,1)} %field_hbm.1, s32[]{:T(128)S(6)} %select_n.3), kind=kLoop, calls=%fused_computation.2 | loop fusion | bytes 131076 | tf_op jit(solution)/shard_map/dynamic_slice | solution.py:319
  0.8 2.0 %collective-permute-start = (bf16[128,256]{1,0:T(8,128)(2,1)S(1)}, bf16[128,256]{1,0:T(8,128)(2,1)S(1)}, u32[]{:S(2)}, u32[]{:S(2)}) collective-permute-start(bf16[128,256]{1,0:T(8,128)(2,1)S(1)} %constant_dynamic-slice_fusion), channel_id=1, source_target_pairs={{0,1},{1,0},{2,3},{3,2},{4,5},{5,4},{6,7},{7,6},{8,9},{9,8},{10,11... | collective-permute-start | bytes 196616 | tf_op jit(solution)/shard_map/ppermute | solution.py:319
  2.9 10.2 %first_step.1 = (bf16[32,6,256,128]{3,2,1,0:T(8,128)(2,1)S(1)}, bf16[2,8704,128]{2,1,0:T(8,128)(2,1)S(1)}, bf16[2,8704,128]{2,1,0:T(8,128)(2,1)S(1)}, f32[8,256]...) custom-call(bf16[24576,128]{1,0:T(8,128)(2,1)} %bitcast.10, bf16[24576,128]{1,0:T(8,128)(2,1)} %bitcast.11, ...), custom_call_target="tpu_custom_call" | custom-call | tf_op jit(solution)/shard_map/first_step/pallas_call | solution.py:323
  13.1 0.0 collective-permute-done.halo_ref
  13.1 0.5 edge_step.3
  13.6 0.1 collective-permute-start.1
  13.7 4.3 %whole_step.3.in_ref = bf16[2,8704,128]{2,1,0:T(8,128)(2,1)S(1)} custom-call(bf16[32,6,256,128]{3,2,1,0:T(8,128)(2,1)S(1)} %get-tuple-element.19.ordered_ref, bf16[2,8704,128]{2,1,0:T(8,128)(2,1)S(1)} %get-tuple-element.24.field_ref, f32[8,256]{1,0:T(8,128)S(1)} %get-tuple-element.21.weight_ref, s32[8,128]{1,0:T(8,128)S(1)} %get-tuple-element.22.floor_ref), custom_call_target="tpu_custom_call" | custom-call | tf_op jit(solution)/shard_map/whole_step/pallas_call | solution.py:372
  18.0 0.0 collective-permute-done.1.halo_ref
  18.0 0.3 edge_step.4
  18.4 2.1 %collective-permute-start.2 = (bf16[128,256]{1,0:T(8,128)(2,1)S(1)}, bf16[128,256]{1,0:T(8,128)(2,1)S(1)}, u32[]{:S(2)}, u32[]{:S(2)}) collective-permute-start(bf16[128,256]{1,0:T(8,128)(2,1)S(1)} %get-tuple-element.27), channel_id=1, source_target_pairs={{0,1},{1,0},{2,3},{3,2},{4,5},{5,4},{6,7},{7,6},{8,9},{9,8},{10,11... | collective-permute-start | bytes 196616 | tf_op jit(solution)/shard_map/ppermute | solution.py:369
  20.5 4.5 %whole_step.4.in_ref = bf16[2,8704,128]{2,1,0:T(8,128)(2,1)S(1)} custom-call(bf16[32,6,256,128]{3,2,1,0:T(8,128)(2,1)S(1)} %get-tuple-element.19.ordered_ref, bf16[2,8704,128]{2,1,0:T(8,128)(2,1)S(1)} %get-tuple-element.26.field_ref, f32[8,256]{1,0:T(8,128)S(1)} %get-tuple-element.21.weight_ref, s32[8,128]{1,0:T(8,128)S(1)} %get-tuple-element.22.floor_ref), custom_call_target="tpu_custom_call" | custom-call | tf_op jit(solution)/shard_map/whole_step/pallas_call | solution.py:372
  25.0 0.0 collective-permute-done.2.halo_ref
  25.0 0.3 edge_step.5
  25.3 0.3 collective-permute-start.3
  25.6 4.1 %whole_step.5.in_ref = f32[2,4104,128]{2,1,0:T(8,128)S(1)} custom-call(bf16[32,6,256,128]{3,2,1,0:T(8,128)(2,1)S(1)} %get-tuple-element.19.ordered_ref, bf16[2,8704,128]{2,1,0:T(8,128)(2,1)S(1)} %get-tuple-element.28.field_ref, f32[8,256]{1,0:T(8,128)S(1)} %get-tuple-element.21.weight_ref, s32[8,128]{1,0:T(8,128)S(1)} %get-tuple-element.22.floor_ref), custom_call_target="tpu_custom_call" | custom-call | tf_op jit(solution)/shard_map/whole_step/pallas_call | solution.py:372
  29.7 0.1 collective-permute-done.3.halo_ref
  29.8 0.0 copy-start
  29.8 1.9 %edge_and_pick.1 = (f32[2,4104,128]{2,1,0:T(8,128)S(1)}, bf16[256,256]{1,0:T(8,128)(2,1)S(1)}, bf16[256,256]{1,0:T(8,128)(2,1)S(1)}) custom-call(bf16[32,6,256,128]{3,2,1,0:T(8,128)(2,1)S(1)} %get-tuple-element.19.ordered_ref, bf16[2,8704,128]{2,1,0:T(8,128)(2,1)S(1)} %get-tuple-element.28.field_ref, ...), custom_call_target="tpu_custom_call", output_to_operand_aliasing={{0}: (5, {})} | custom-call | tf_op jit(solution)/shard_map/edge_and_pick/pallas_call | solution.py:382
  31.8 2.0 %collective-permute-start.4 = (bf16[256,256]{1,0:T(8,128)(2,1)S(1)}, bf16[256,256]{1,0:T(8,128)(2,1)S(1)}, u32[]{:S(2)}, u32[]{:S(2)}) collective-permute-start(bf16[256,256]{1,0:T(8,128)(2,1)S(1)} %get-tuple-element.32), channel_id=1, source_target_pairs={{0,1},{1,0},{2,3},{3,2},{4,5},{5,4},{6,7},{7,6},{8,9},{9,8},{10,11... | collective-permute-start | bytes 393224 | tf_op jit(solution)/shard_map/ppermute | solution.py:398
  33.7 0.0 collective-permute-start.5
  33.7 3.1 %collective-permute-done.4.got_ref = bf16[256,256]{1,0:T(8,128)(2,1)S(1)} collective-permute-done((bf16[256,256]{1,0:T(8,128)(2,1)S(1)}, bf16[256,256]{1,0:T(8,128)(2,1)S(1)}, u32[]{:S(2)}, u32[]{:S(2)}) %collective-permute-start.4) | collective-permute-done | bytes 131104 | tf_op jit(solution)/shard_map/ppermute | solution.py:398
  36.8 0.0 collective-permute-start.6
  36.8 0.0 copy-done
  36.8 0.5 basis.1.basis_ref
  37.4 0.0 collective-permute-done.5.keep2_ref
  37.4 0.8 %collective-permute-done.6.got2_ref = bf16[256,256]{1,0:T(8,128)(2,1)S(1)} collective-permute-done((bf16[256,256]{1,0:T(8,128)(2,1)S(1)}, bf16[256,256]{1,0:T(8,128)(2,1)S(1)}, u32[]{:S(2)}, u32[]{:S(2)}) %collective-permute-start.6) | collective-permute-done | bytes 131104 | tf_op jit(solution)/shard_map/ppermute | solution.py:409
  38.2 0.5 series.1
  38.6 24.3 %all_to_all.5 = bf16[32,32,256]{2,1,0:T(8,128)(2,1)S(1)} all-to-all(bf16[32,32,256]{2,1,0:T(8,128)(2,1)S(1)} %bitcast.8), channel_id=1, replica_groups=mesh['x'=4,'y'=4,'zh'=2,'core'=2,'depth'=2] {'x','y','zh'}, dimensions={0} | all-to-all | bytes 1048576 | tf_op jit(solution)/shard_map/all_to_all | solution.py:420
  62.9 0.1 convert_reduce_fusion
  63.0 0.6 multiply_bitcast_fusion
Async XLA Ops:
  0.8 12.2 %collective-permute-start = (bf16[128,256]{1,0:T(8,128)(2,1)S(1)}, bf16[128,256]{1,0:T(8,128)(2,1)S(1)}, u32[]{:S(2)}, u32[]{:S(2)}) collective-permute-start(bf16[128,256]{1,0:T(8,128)(2,1)S(1)} %constant_dynamic-slice_fusion), channel_id=1, source_target_pairs={{0,1},{1,0},{2,3},{3,2},{4,5},{5,4},{6,7},{7,6},{8,9},{9,8},{10,11... | collective-permute-start | bytes 196616 | tf_op jit(solution)/shard_map/ppermute | solution.py:319
  13.6 4.5 %collective-permute-start.1 = (bf16[128,256]{1,0:T(8,128)(2,1)S(1)}, bf16[128,256]{1,0:T(8,128)(2,1)S(1)}, u32[]{:S(2)}, u32[]{:S(2)}) collective-permute-start(bf16[128,256]{1,0:T(8,128)(2,1)S(1)} %get-tuple-element.25), channel_id=1, source_target_pairs={{0,1},{1,0},{2,3},{3,2},{4,5},{5,4},{6,7},{7,6},{8,9},{9,8},{10,11... | collective-permute-start | bytes 196616 | tf_op jit(solution)/shard_map/ppermute | solution.py:369
  18.4 6.6 %collective-permute-start.2 = (bf16[128,256]{1,0:T(8,128)(2,1)S(1)}, bf16[128,256]{1,0:T(8,128)(2,1)S(1)}, u32[]{:S(2)}, u32[]{:S(2)}) collective-permute-start(bf16[128,256]{1,0:T(8,128)(2,1)S(1)} %get-tuple-element.27), channel_id=1, source_target_pairs={{0,1},{1,0},{2,3},{3,2},{4,5},{5,4},{6,7},{7,6},{8,9},{9,8},{10,11... | collective-permute-start | bytes 196616 | tf_op jit(solution)/shard_map/ppermute | solution.py:369
  25.3 4.5 %collective-permute-start.3 = (bf16[128,256]{1,0:T(8,128)(2,1)S(1)}, bf16[128,256]{1,0:T(8,128)(2,1)S(1)}, u32[]{:S(2)}, u32[]{:S(2)}) collective-permute-start(bf16[128,256]{1,0:T(8,128)(2,1)S(1)} %get-tuple-element.29), channel_id=1, source_target_pairs={{0,1},{1,0},{2,3},{3,2},{4,5},{5,4},{6,7},{7,6},{8,9},{9,8},{10,11... | collective-permute-start | bytes 196616 | tf_op jit(solution)/shard_map/ppermute | solution.py:369
  29.8 7.0 %copy-start = (f32[8192]{0:T(1024)S(1)}, f32[8192]{0:T(1024)}, u32[]{:S(2)}) copy-start(f32[8192]{0:T(1024)} %param.11) | copy-start | bytes 98308
  31.8 5.0 %collective-permute-start.4 = (bf16[256,256]{1,0:T(8,128)(2,1)S(1)}, bf16[256,256]{1,0:T(8,128)(2,1)S(1)}, u32[]{:S(2)}, u32[]{:S(2)}) collective-permute-start(bf16[256,256]{1,0:T(8,128)(2,1)S(1)} %get-tuple-element.32), channel_id=1, source_target_pairs={{0,1},{1,0},{2,3},{3,2},{4,5},{5,4},{6,7},{7,6},{8,9},{9,8},{10,11... | collective-permute-start | bytes 393224 | tf_op jit(solution)/shard_map/ppermute | solution.py:398
  33.7 3.6 %collective-permute-start.5 = (bf16[256,256]{1,0:T(8,128)(2,1)S(1)}, bf16[256,256]{1,0:T(8,128)(2,1)S(1)}, u32[]{:S(2)}, u32[]{:S(2)}) collective-permute-start(bf16[256,256]{1,0:T(8,128)(2,1)S(1)} %get-tuple-element.31.keep_ref), channel_id=1, source_target_pairs={{0,2},{2,0},{1,3},{3,1},{4,6},{6,4},{5,7},{7,5},{8,10},{10,8},{9,1... | collective-permute-start | bytes 393224 | tf_op jit(solution)/shard_map/ppermute | solution.py:399
  36.8 1.3 %collective-permute-start.6 = (bf16[256,256]{1,0:T(8,128)(2,1)S(1)}, bf16[256,256]{1,0:T(8,128)(2,1)S(1)}, u32[]{:S(2)}, u32[]{:S(2)}) collective-permute-start(bf16[256,256]{1,0:T(8,128)(2,1)S(1)} %collective-permute-done.4.got_ref), channel_id=1, source_target_pairs={{0,2},{2,0},{1,3},{3,1},{4,6},{6,4},{5,7},{7,5},{8,10},{10,8},{9,1... | collective-permute-start | bytes 393224 | tf_op jit(solution)/shard_map/ppermute | solution.py:409

commit v3 on v2

--- a/solution.py
+++ b/solution.py
@@ -7,14 +7,15 @@
 from jax.experimental.pallas import tpu as pltpu
 from jax.sharding import Mesh, PartitionSpec as P
 
+
 NT = 2048
 STEPS = 4
 BS = 128
 F32 = jnp.float32
 BF16 = jnp.bfloat16
 CHUNKS = 8
-AHEAD = 2
-UNROLL = 8
+AHEAD = 3
+UNROLL = 32
 
 VMEM_SPEC = pl.BlockSpec(memory_space=pltpu.VMEM)
 HBM_SPEC = pl.BlockSpec(memory_space=pl.ANY)
@@ -90,10 +91,10 @@
     ref[:, ref.shape[1] - 2 * BS :, :] = edge
 
 
-def first_step(
+def load(
     main_hbm, side_hbm, field_hbm, coupling_hbm, floors_hbm,
-    receivers_hbm, ordered_ref, start_ref, next_ref, weight_ref, floor_ref, pick_ref,
-    main_buf, side_buf, field_buf, planes, coupling_buf, floors_buf, receivers_buf, sems, small_sems,
+    receivers_hbm, ordered_ref, start_ref, edge_ref, weight_ref, floor_ref, pick_ref,
+    main_buf, side_buf, field_buf, planes, perm_ref, coupling_buf, floors_buf, receivers_buf, sems, small_sems,
 ):
     blocks = ordered_ref.shape[0]
     per = blocks // CHUNKS
@@ -118,75 +119,61 @@
                 )
             ]
         )
-    copies[0][0].start()
     for n in range(AHEAD):
-        copies[n + 1][0].start()
-        copies[n][1].start()
-        copies[n][2].start()
-    perm = split_matrix(width)
-    for ref in (start_ref, next_ref):
-        zero_ends(ref)
-    coupling_copy.wait()
-    floors_copy.wait()
-    weights = jnp.dot(
-        jnp.broadcast_to(coupling_buf[...], (8, width)), perm, preferred_element_type=F32, precision=lax.Precision.HIGHEST
-    )
-    weight_ref[...] = weights
-    perm = perm.astype(BF16)
+        for kind in range(3):
+            copies[n][kind].start()
+    perm_ref[...] = split_matrix(width).astype(BF16)
     first_row = lax.axis_index("depth") * (blocks * BS)
-    lanes = floor_ref.shape
-    floors = jnp.zeros(lanes, jnp.int32)
-    for step in range(STEPS):
-        floors = jnp.where(lax.broadcasted_iota(jnp.int32, lanes, 0) == step, floors_buf[step] - first_row, floors)
-    floor_ref[...] = floors
-    receivers_copy.wait()
-    local = receivers_buf[...] - first_row
-    pick_ref[...] = jnp.where(jnp.logical_and(local >= 0, local < blocks * BS), local, blocks * BS)
+
+    def small_tables():
+        zero_ends(start_ref)
+        weight_ref[...] = jnp.dot(
+            jnp.broadcast_to(coupling_buf[...], (8, width)),
+            split_matrix(width),
+            preferred_element_type=F32,
+            precision=lax.Precision.HIGHEST,
+        )
+        shape = floor_ref.shape
+        floors = jnp.zeros(shape, jnp.int32)
+        for step in range(STEPS):
+            floors = jnp.where(lax.broadcasted_iota(jnp.int32, shape, 0) == step, floors_buf[step] - first_row, floors)
+        floor_ref[...] = floors
+        local = receivers_buf[...] - first_row
+        local = jnp.where(jnp.logical_and(local >= 0, local < blocks * BS), local, blocks * BS)
+        mine = local.shape[0] // 2
+        turned = jnp.concatenate([local[mine:], local[:mine]], axis=0)
+        pick_ref[...] = jnp.where(lax.axis_index("depth") == 0, turned, local)
 
     def split_chunk(n):
         for j in range(per):
             b = n * per + j
-            field = jnp.dot(field_buf[b * BS : (b + 1) * BS, :], perm, preferred_element_type=F32).astype(BF16)
+            field = jnp.dot(field_buf[b * BS : (b + 1) * BS, :], perm_ref[...], preferred_element_type=F32).astype(BF16)
             put_block(start_ref, b + 1, field)
 
-    def order_block(n, j):
+    def order_block(n, j, kind):
         b = n * per + j
-        for kind, buf in enumerate((main_buf, side_buf)):
-            plane = planes.at[(n % 2) * 2 * per + j * 2 + kind]
-            plane[...] = buf[b * BS * 6 : (b + 1) * BS * 6, :].astype(F32)
-            for m in range(6):
-                ordered_ref[b, m, kind * BS : (kind + 1) * BS, :] = plane[pl.ds(m, BS, stride=6), :].astype(BF16)
-
-    def march_block(b):
-        field = advanced(
-            operator_rows(ordered_ref, b), three_blocks(start_ref, b), weights, b * BS, floors[0:1, : width // 2]
-        )
-        put_block(next_ref, b + 1, field)
-
-    always = lax.axis_index("depth") >= 0
-    copies[0][0].wait()
-    split_chunk(0)
-    for n in range(CHUNKS + 1):
-        if n < CHUNKS:
-            copies[n][1].wait()
-            copies[n][2].wait()
+        buf = (main_buf, side_buf)[kind]
+        plane = planes.at[(n % 2) * 2 * per + j * 2 + kind]
+        plane[...] = buf[b * BS * 6 : (b + 1) * BS * 6, :].astype(F32)
+        for m in range(6):
+            ordered_ref[b, m, kind * BS : (kind + 1) * BS, :] = plane[pl.ds(m, BS, stride=6), :].astype(BF16)
+
+    for n in range(CHUNKS):
+        for kind in range(3):
+            copies[n][kind].wait()
             if n + AHEAD < CHUNKS:
-                copies[n + AHEAD][1].start()
-                copies[n + AHEAD][2].start()
-                if n + AHEAD + 1 < CHUNKS:
-                    copies[n + AHEAD + 1][0].start()
-            if n + 1 < CHUNKS:
-                copies[n + 1][0].wait()
-
-        @pl.when(always)
-        def _(n=n):
-            for j in range(per):
-                if n > 0:
-                    march_block((n - 1) * per + j)
-                if n < CHUNKS:
-                    order_block(n, j)
-            if n + 1 < CHUNKS:
-                split_chunk(n + 1)
+                copies[n + AHEAD][kind].start()
+        split_chunk(n)
+        for j in range(per):
+            order_block(n, j, 0)
+            order_block(n, j, 1)
+        if n == 1:
+            coupling_copy.wait()
+            floors_copy.wait()
+            receivers_copy.wait()
+            small_tables()
+    edge_at = pl.multiple_of((1 + (blocks - 1) * (1 - lax.axis_index("depth"))) * 2 * BS, 2 * BS)
+    edge_ref[...] = jnp.concatenate([start_ref[0, pl.ds(edge_at, BS), :], start_ref[1, pl.ds(edge_at, BS), :]], axis=1)
 
 
 def whole_step(step, last):
@@ -219,8 +206,6 @@
     blocks = ordered_ref.shape[0]
     side = lax.axis_index("depth")
     halo = halo_ref[...]
-    if step == 0:
-        halo = jnp.dot(halo, split_matrix(halo.shape[1]).astype(BF16), preferred_element_type=F32).astype(BF16)
     b = (blocks - 1) * (1 - side)
     size = 2 * BS
     at = pl.multiple_of(b * size, size)
@@ -253,21 +238,14 @@
     rows_copy.start()
     b, field = edge_block(STEPS - 1, ordered_ref, field_ref, weight_ref, floor_ref, halo_ref, halo_buf)
     put_final(final_ref, pl.multiple_of(b * BS, BS), field)
-    side = lax.axis_index("depth")
     owned = keep_ref.shape[0]
     lanes = rows_ref.shape[1]
-    group = 32
     rows_copy.wait()
-    for out_ref, owner in ((send_ref, 1 - side), (keep_ref, side)):
-
-        def some(n, carry):
-            for j in range(group):
-                at = rows_ref[owner * (owned // lanes) + n // (lanes // group), (n % (lanes // group)) * group + j]
-                picked[0, pl.ds(n * group + j, 1), :] = final_ref[0, pl.ds(at, 1), :]
-                picked[1, pl.ds(n * group + j, 1), :] = final_ref[1, pl.ds(at, 1), :]
-            return carry
-
-        lax.fori_loop(0, owned // group, some, 0)
+    for which, out_ref in enumerate((send_ref, keep_ref)):
+        for n in range(owned):
+            at = rows_ref[(which * owned + n) // lanes, n % lanes]
+            for part in range(2):
+                picked[part, n : n + 1, :] = final_ref[part, pl.ds(at, 1), :]
         out_ref[...] = jnp.concatenate([picked[0], picked[1]], axis=1).astype(BF16)
 
 
@@ -314,18 +292,15 @@
 def local(pressure_field, block_main, block_coupled, coupling, frequencies, receivers, floors):
     rows, width = pressure_field.shape
     blocks = rows // BS
-    side = lax.axis_index("depth")
     swap = [(0, 1), (1, 0)]
-    halo = lax.ppermute(lax.dynamic_slice_in_dim(pressure_field, (1 - side) * (rows - BS), BS, 0), "depth", swap)
-
     padded = (2, (blocks + 2) * 2 * BS, width // 2)
     halo_buf = pltpu.VMEM((2, 6 * BS, width // 2), BF16)
-    ordered, start, field, weights, floor_rows, pick_rows = pl.pallas_call(
-        first_step,
+    ordered, start, edge, weights, floor_rows, pick_rows = pl.pallas_call(
+        load,
         out_shape=(
             vmem((blocks, 6, 2 * BS, BS), BF16),
             vmem(padded, BF16),
-            vmem(padded, BF16),
+            vmem((BS, width), BF16),
             vmem((8, width), F32),
             vmem((8, width // 2), jnp.int32),
             vmem((receivers.shape[0] // BS, BS), jnp.int32),
@@ -337,6 +312,7 @@
             pltpu.VMEM((rows * 6, BS), BF16),
             pltpu.VMEM((rows, width), BF16),
             pltpu.VMEM((4 * blocks // CHUNKS, BS * 6, BS), F32),
+            pltpu.VMEM((width, width), BF16),
             pltpu.VMEM((1, width), F32),
             pltpu.SMEM((STEPS,), jnp.int32),
             pltpu.VMEM((receivers.shape[0] // BS, BS), jnp.int32),
@@ -344,7 +320,7 @@
             pltpu.SemaphoreType.DMA((3,)),
         ],
         compiler_params=limit(28),
-        name="first_step",
+        name="load",
     )(
         in_hbm(block_main.reshape(rows * 6, BS)),
         in_hbm(block_coupled.reshape(rows * 6, BS)),
@@ -355,8 +331,20 @@
     )
 
     before = start
-    for step in range(STEPS - 1):
-        field, edge = pl.pallas_call(
+    for step in range(STEPS):
+        last = step == STEPS - 1
+        halo = lax.ppermute(edge, "depth", swap)
+        field = pl.pallas_call(
+            whole_step(step, last),
+            out_shape=vmem((2, rows + 8, width // 2), F32) if last else vmem(padded, BF16),
+            in_specs=[VMEM_SPEC] * 4,
+            out_specs=VMEM_SPEC,
+            compiler_params=limit(6),
+            name="whole_step",
+        )(ordered, before, weights, floor_rows)
+        if last:
+            break
+        before, edge = pl.pallas_call(
             edge_step(step),
             out_shape=(vmem(padded, BF16), vmem((BS, width), BF16)),
             in_specs=[VMEM_SPEC] * 6,
@@ -366,17 +354,6 @@
             compiler_params=limit(6),
             name="edge_step",
         )(ordered, before, weights, floor_rows, halo, field)
-        halo = lax.ppermute(edge, "depth", swap)
-        last = step == STEPS - 2
-        before = field
-        field = pl.pallas_call(
-            whole_step(step + 1, last),
-            out_shape=vmem((2, rows + 8, width // 2), F32) if last else vmem(padded, BF16),
-            in_specs=[VMEM_SPEC] * 4,
-            out_specs=VMEM_SPEC,
-            compiler_params=limit(6),
-            name="whole_step",
-        )(ordered, before, weights, floor_rows)
 
     owned = receivers.shape[0] // lax.axis_size("depth")
     _, keep, send = pl.pallas_call(
@@ -403,7 +380,6 @@
         in_specs=[VMEM_SPEC],
         out_specs=VMEM_SPEC,
         compiler_params=limit(8),
-        cost_estimate=pl.CostEstimate(flops=4_000_000_000, bytes_accessed=0, transcendentals=0),
         name="basis",
     )(frequencies.reshape(-1, width // 2))
     got2 = lax.ppermute(got, "core", swap)
@@ -436,4 +412,5 @@
         P(),
         P(),
     )
+
     return jax.shard_map(local, mesh=chips, in_specs=in_specs, out_specs=P("depth", freq), check_vma=False)

time: 63.8 us -> 60.2 us (0.944)
  Pallas kernels: 27.2 us -> 24.1 us
  local copies, waits for them, and re-layouts: 0.85 us -> 0.01 us
    ppermute x3 -> x4, starting transfers between devices: 2.45 us -> 5.25 us  [local(): halo = lax.ppermute(edge, 'depth', swap)]
    pallas_call x4 -> x5, Pallas kernels: 23.1 us -> 20.9 us  [the longest x4 14.3 us: local(): pl.pallas_call(whole_step(step, last), out_shape=vmem((2, rows + 8, width...]
    ppermute x1 -> x0, starting transfers between devices: 2.03 us -> none  [local(): lax.ppermute(lax.dynamic_slice_in_dim(pressure_field, (1 - side) * (rows...]
    dynamic_slice x1 -> x0, local copies, waits for them, and re-layouts: 0.84 us -> none  [local(): lax.dynamic_slice_in_dim(pressure_field, (1 - side) * (rows - BS), BS, 0)]
    pallas_call x1, Pallas kernels: 1.92 us -> 1.18 us  [local(): pl.pallas_call(edge_and_pick, out_shape=(vmem((2, rows + 8, width // 2),...]
  transfers between devices with their start and end apart: 7 -> 7, of which waited for: 3 -> 2; matrix products, arithmetic and copies ran while one was open for 0% -> 0% of each run, Pallas kernels for 37% -> 25%
where the time goes in v3:
time: 60.2 us; the launch traced here: 60.1 us
  Pallas kernels  24.1 us (40%)
  blocking collectives  24 us (40%)
  starting transfers between devices  6.65 us (11%)
  waiting for transfers between devices  4.51 us (7%)
  other arithmetic  0.7 us (1%)
    all_to_all x1, blocking collectives, local(): lax.all_to_all(partial.reshape(groups, NT // 2 // groups, owned), others,...  24 us
    pallas_call x4, Pallas kernels, local(): pl.pallas_call(whole_step(step, last), out_shape=vmem((2, rows + 8, width...  14.3 us
    pallas_call x1, Pallas kernels, local(): pl.pallas_call(load, out_shape=(vmem((blocks, 6, 2 * BS, BS), BF16), vmem...  6.59 us
    ppermute x4, starting transfers between devices, local(): halo = lax.ppermute(edge, 'depth', swap)  5.25 us
    ppermute x1, waiting for transfers between devices, local(): got = lax.ppermute(send, 'depth', swap)  3.65 us
    ppermute x1, starting transfers between devices, local(): got = lax.ppermute(send, 'depth', swap)  1.39 us
  transfers between devices with their start and end apart: 7, of which 2 were waited for; matrix products, arithmetic and copies ran while one was open for 0% of the time, Pallas kernels for 25%

profile of v3, /device:TPU:0, one launch (start us, length us, event | category | flops | bytes accessed | tf_op | source)
XLA Modules:
  0.0 60.1 jit_solution(3239286311385595736)
XLA Ops:
  0.0 6.6 %load.1 = (bf16[32,6,256,128]{3,2,1,0:T(8,128)(2,1)S(1)}, bf16[2,8704,128]{2,1,0:T(8,128)(2,1)S(1)}, bf16[128,256]{1,0:T(8,128)(2,1)S(1)}, f32[8,256]{1,0:T(8,12...) custom-call(bf16[24576,128]{1,0:T(8,128)(2,1)} %bitcast.10, bf16[24576,128]{1,0:T(8,128)(2,1)} %bitcast.11, ...), custom_call_target="tpu_custom_call" | custom-call | tf_op jit(solution)/shard_map/load/pallas_call | solution.py:298
  6.6 2.1 %collective-permute-start = (bf16[128,256]{1,0:T(8,128)(2,1)S(1)}, bf16[128,256]{1,0:T(8,128)(2,1)S(1)}, u32[]{:S(2)}, u32[]{:S(2)}) collective-permute-start(bf16[128,256]{1,0:T(8,128)(2,1)S(1)} %get-tuple-element.23), channel_id=1, source_target_pairs={{0,1},{1,0},{2,3},{3,2},{4,5},{5,4},{6,7},{7,6},{8,9},{9,8},{10,11... | collective-permute-start | bytes 196616 | tf_op jit(solution)/shard_map/ppermute | solution.py:336
  8.7 3.5 %whole_step.4.in_ref = bf16[2,8704,128]{2,1,0:T(8,128)(2,1)S(1)} custom-call(bf16[32,6,256,128]{3,2,1,0:T(8,128)(2,1)S(1)} %get-tuple-element.19.ordered_ref, bf16[2,8704,128]{2,1,0:T(8,128)(2,1)S(1)} %get-tuple-element.20.field_ref, f32[8,256]{1,0:T(8,128)S(1)} %get-tuple-element.21.weight_ref, s32[8,128]{1,0:T(8,128)S(1)} %get-tuple-element.22.floor_ref), custom_call_target="tpu_custom_call" | custom-call | tf_op jit(solution)/shard_map/whole_step/pallas_call | solution.py:337
  12.2 0.0 collective-permute-done.halo_ref
  12.3 0.3 edge_step.3
  12.6 0.8 %collective-permute-start.1 = (bf16[128,256]{1,0:T(8,128)(2,1)S(1)}, bf16[128,256]{1,0:T(8,128)(2,1)S(1)}, u32[]{:S(2)}, u32[]{:S(2)}) collective-permute-start(bf16[128,256]{1,0:T(8,128)(2,1)S(1)} %get-tuple-element.25), channel_id=1, source_target_pairs={{0,1},{1,0},{2,3},{3,2},{4,5},{5,4},{6,7},{7,6},{8,9},{9,8},{10,11... | collective-permute-start | bytes 196616 | tf_op jit(solution)/shard_map/ppermute | solution.py:336
  13.4 3.5 %whole_step.5.in_ref = bf16[2,8704,128]{2,1,0:T(8,128)(2,1)S(1)} custom-call(bf16[32,6,256,128]{3,2,1,0:T(8,128)(2,1)S(1)} %get-tuple-element.19.ordered_ref, bf16[2,8704,128]{2,1,0:T(8,128)(2,1)S(1)} %get-tuple-element.24.field_ref, f32[8,256]{1,0:T(8,128)S(1)} %get-tuple-element.21.weight_ref, s32[8,128]{1,0:T(8,128)S(1)} %get-tuple-element.22.floor_ref), custom_call_target="tpu_custom_call" | custom-call | tf_op jit(solution)/shard_map/whole_step/pallas_call | solution.py:337
  16.9 0.0 collective-permute-done.1.halo_ref
  16.9 0.3 edge_step.4
  17.3 1.6 %collective-permute-start.2 = (bf16[128,256]{1,0:T(8,128)(2,1)S(1)}, bf16[128,256]{1,0:T(8,128)(2,1)S(1)}, u32[]{:S(2)}, u32[]{:S(2)}) collective-permute-start(bf16[128,256]{1,0:T(8,128)(2,1)S(1)} %get-tuple-element.27), channel_id=1, source_target_pairs={{0,1},{1,0},{2,3},{3,2},{4,5},{5,4},{6,7},{7,6},{8,9},{9,8},{10,11... | collective-permute-start | bytes 196616 | tf_op jit(solution)/shard_map/ppermute | solution.py:336
  18.9 3.7 %whole_step.6.in_ref = bf16[2,8704,128]{2,1,0:T(8,128)(2,1)S(1)} custom-call(bf16[32,6,256,128]{3,2,1,0:T(8,128)(2,1)S(1)} %get-tuple-element.19.ordered_ref, bf16[2,8704,128]{2,1,0:T(8,128)(2,1)S(1)} %get-tuple-element.26.field_ref, f32[8,256]{1,0:T(8,128)S(1)} %get-tuple-element.21.weight_ref, s32[8,128]{1,0:T(8,128)S(1)} %get-tuple-element.22.floor_ref), custom_call_target="tpu_custom_call" | custom-call | tf_op jit(solution)/shard_map/whole_step/pallas_call | solution.py:337
  22.6 0.0 collective-permute-done.2.halo_ref
  22.6 0.3 edge_step.5
  22.9 0.8 %collective-permute-start.3 = (bf16[128,256]{1,0:T(8,128)(2,1)S(1)}, bf16[128,256]{1,0:T(8,128)(2,1)S(1)}, u32[]{:S(2)}, u32[]{:S(2)}) collective-permute-start(bf16[128,256]{1,0:T(8,128)(2,1)S(1)} %get-tuple-element.29), channel_id=1, source_target_pairs={{0,1},{1,0},{2,3},{3,2},{4,5},{5,4},{6,7},{7,6},{8,9},{9,8},{10,11... | collective-permute-start | bytes 196616 | tf_op jit(solution)/shard_map/ppermute | solution.py:336
  23.7 3.5 %whole_step.7.in_ref = f32[2,4104,128]{2,1,0:T(8,128)S(1)} custom-call(bf16[32,6,256,128]{3,2,1,0:T(8,128)(2,1)S(1)} %get-tuple-element.19.ordered_ref, bf16[2,8704,128]{2,1,0:T(8,128)(2,1)S(1)} %get-tuple-element.28.field_ref, f32[8,256]{1,0:T(8,128)S(1)} %get-tuple-element.21.weight_ref, s32[8,128]{1,0:T(8,128)S(1)} %get-tuple-element.22.floor_ref), custom_call_target="tpu_custom_call" | custom-call | tf_op jit(solution)/shard_map/whole_step/pallas_call | solution.py:337
  27.2 0.0 collective-permute-done.3.halo_ref
  27.3 0.0 copy-start
  27.3 1.2 %edge_and_pick.1 = (f32[2,4104,128]{2,1,0:T(8,128)S(1)}, bf16[256,256]{1,0:T(8,128)(2,1)S(1)}, bf16[256,256]{1,0:T(8,128)(2,1)S(1)}) custom-call(bf16[32,6,256,128]{3,2,1,0:T(8,128)(2,1)S(1)} %get-tuple-element.19.ordered_ref, bf16[2,8704,128]{2,1,0:T(8,128)(2,1)S(1)} %get-tuple-element.28.field_ref, ...), custom_call_target="tpu_custom_call", output_to_operand_aliasing={{0}: (5, {})} | custom-call | tf_op jit(solution)/shard_map/edge_and_pick/pallas_call | solution.py:359
  28.5 1.4 %collective-permute-start.4 = (bf16[256,256]{1,0:T(8,128)(2,1)S(1)}, bf16[256,256]{1,0:T(8,128)(2,1)S(1)}, u32[]{:S(2)}, u32[]{:S(2)}) collective-permute-start(bf16[256,256]{1,0:T(8,128)(2,1)S(1)} %get-tuple-element.32), channel_id=1, source_target_pairs={{0,1},{1,0},{2,3},{3,2},{4,5},{5,4},{6,7},{7,6},{8,9},{9,8},{10,11... | collective-permute-start | bytes 393224 | tf_op jit(solution)/shard_map/ppermute | solution.py:375
  29.9 0.0 collective-permute-start.5
  29.9 3.7 %collective-permute-done.4.got_ref = bf16[256,256]{1,0:T(8,128)(2,1)S(1)} collective-permute-done((bf16[256,256]{1,0:T(8,128)(2,1)S(1)}, bf16[256,256]{1,0:T(8,128)(2,1)S(1)}, u32[]{:S(2)}, u32[]{:S(2)}) %collective-permute-start.4) | collective-permute-done | bytes 131104 | tf_op jit(solution)/shard_map/ppermute | solution.py:375
  33.5 0.0 collective-permute-start.6
  33.5 0.0 copy-done
  33.5 0.5 basis.1.basis_ref
  34.1 0.0 collective-permute-done.5.keep2_ref
  34.1 0.8 %collective-permute-done.6.got2_ref = bf16[256,256]{1,0:T(8,128)(2,1)S(1)} collective-permute-done((bf16[256,256]{1,0:T(8,128)(2,1)S(1)}, bf16[256,256]{1,0:T(8,128)(2,1)S(1)}, u32[]{:S(2)}, u32[]{:S(2)}) %collective-permute-start.6) | collective-permute-done | bytes 131104 | tf_op jit(solution)/shard_map/ppermute | solution.py:385
  34.9 0.5 series.1
  35.4 24.0 %all_to_all.5 = bf16[32,32,256]{2,1,0:T(8,128)(2,1)S(1)} all-to-all(bf16[32,32,256]{2,1,0:T(8,128)(2,1)S(1)} %bitcast.8), channel_id=1, replica_groups=mesh['x'=4,'y'=4,'zh'=2,'core'=2,'depth'=2] {'x','y','zh'}, dimensions={0} | all-to-all | bytes 1048576 | tf_op jit(solution)/shard_map/all_to_all | solution.py:396
  59.4 0.1 convert_reduce_fusion
  59.4 0.6 %multiply_bitcast_fusion = f32[256,32]{0,1:T(8,128)} fusion(f32[32,256]{1,0:T(8,128)S(1)} %convert_reduce_fusion), kind=kLoop, calls=%fused_computation.1 | loop fusion | flops 8192 | bytes 65536 | tf_op jit(solution)/shard_map/mul | solution.py:399
Async XLA Ops:
  6.6 5.7 %collective-permute-start = (bf16[128,256]{1,0:T(8,128)(2,1)S(1)}, bf16[128,256]{1,0:T(8,128)(2,1)S(1)}, u32[]{:S(2)}, u32[]{:S(2)}) collective-permute-start(bf16[128,256]{1,0:T(8,128)(2,1)S(1)} %get-tuple-element.23), channel_id=1, source_target_pairs={{0,1},{1,0},{2,3},{3,2},{4,5},{5,4},{6,7},{7,6},{8,9},{9,8},{10,11... | collective-permute-start | bytes 196616 | tf_op jit(solution)/shard_map/ppermute | solution.py:336
  12.6 4.3 %collective-permute-start.1 = (bf16[128,256]{1,0:T(8,128)(2,1)S(1)}, bf16[128,256]{1,0:T(8,128)(2,1)S(1)}, u32[]{:S(2)}, u32[]{:S(2)}) collective-permute-start(bf16[128,256]{1,0:T(8,128)(2,1)S(1)} %get-tuple-element.25), channel_id=1, source_target_pairs={{0,1},{1,0},{2,3},{3,2},{4,5},{5,4},{6,7},{7,6},{8,9},{9,8},{10,11... | collective-permute-start | bytes 196616 | tf_op jit(solution)/shard_map/ppermute | solution.py:336
  17.3 5.3 %collective-permute-start.2 = (bf16[128,256]{1,0:T(8,128)(2,1)S(1)}, bf16[128,256]{1,0:T(8,128)(2,1)S(1)}, u32[]{:S(2)}, u32[]{:S(2)}) collective-permute-start(bf16[128,256]{1,0:T(8,128)(2,1)S(1)} %get-tuple-element.27), channel_id=1, source_target_pairs={{0,1},{1,0},{2,3},{3,2},{4,5},{5,4},{6,7},{7,6},{8,9},{9,8},{10,11... | collective-permute-start | bytes 196616 | tf_op jit(solution)/shard_map/ppermute | solution.py:336
  22.9 4.3 %collective-permute-start.3 = (bf16[128,256]{1,0:T(8,128)(2,1)S(1)}, bf16[128,256]{1,0:T(8,128)(2,1)S(1)}, u32[]{:S(2)}, u32[]{:S(2)}) collective-permute-start(bf16[128,256]{1,0:T(8,128)(2,1)S(1)} %get-tuple-element.29), channel_id=1, source_target_pairs={{0,1},{1,0},{2,3},{3,2},{4,5},{5,4},{6,7},{7,6},{8,9},{9,8},{10,11... | collective-permute-start | bytes 196616 | tf_op jit(solution)/shard_map/ppermute | solution.py:336
  27.3 6.2 %copy-start = (f32[8192]{0:T(1024)S(1)}, f32[8192]{0:T(1024)}, u32[]{:S(2)}) copy-start(f32[8192]{0:T(1024)} %param.11) | copy-start | bytes 98308
  28.5 5.0 %collective-permute-start.4 = (bf16[256,256]{1,0:T(8,128)(2,1)S(1)}, bf16[256,256]{1,0:T(8,128)(2,1)S(1)}, u32[]{:S(2)}, u32[]{:S(2)}) collective-permute-start(bf16[256,256]{1,0:T(8,128)(2,1)S(1)} %get-tuple-element.32), channel_id=1, source_target_pairs={{0,1},{1,0},{2,3},{3,2},{4,5},{5,4},{6,7},{7,6},{8,9},{9,8},{10,11... | collective-permute-start | bytes 393224 | tf_op jit(solution)/shard_map/ppermute | solution.py:375
  29.9 4.2 %collective-permute-start.5 = (bf16[256,256]{1,0:T(8,128)(2,1)S(1)}, bf16[256,256]{1,0:T(8,128)(2,1)S(1)}, u32[]{:S(2)}, u32[]{:S(2)}) collective-permute-start(bf16[256,256]{1,0:T(8,128)(2,1)S(1)} %get-tuple-element.31.keep_ref), channel_id=1, source_target_pairs={{0,2},{2,0},{1,3},{3,1},{4,6},{6,4},{5,7},{7,5},{8,10},{10,8},{9,1... | collective-permute-start | bytes 393224 | tf_op jit(solution)/shard_map/ppermute | solution.py:376
  33.5 1.3 %collective-permute-start.6 = (bf16[256,256]{1,0:T(8,128)(2,1)S(1)}, bf16[256,256]{1,0:T(8,128)(2,1)S(1)}, u32[]{:S(2)}, u32[]{:S(2)}) collective-permute-start(bf16[256,256]{1,0:T(8,128)(2,1)S(1)} %collective-permute-done.4.got_ref), channel_id=1, source_target_pairs={{0,2},{2,0},{1,3},{3,1},{4,6},{6,4},{5,7},{7,5},{8,10},{10,8},{9,1... | collective-permute-start | bytes 393224 | tf_op jit(solution)/shard_map/ppermute | solution.py:385

commit v4 on v3

--- a/solution.py
+++ b/solution.py
@@ -13,9 +13,8 @@
 BS = 128
 F32 = jnp.float32
 BF16 = jnp.bfloat16
-CHUNKS = 8
+CHUNKS = (1, 3, 4, 4, 4, 4, 4, 4, 2, 2)
 AHEAD = 3
-UNROLL = 32
 
 VMEM_SPEC = pl.BlockSpec(memory_space=pltpu.VMEM)
 HBM_SPEC = pl.BlockSpec(memory_space=pl.ANY)
@@ -65,7 +64,10 @@
 
 
 def advanced(ordered, stacked, weights, first_row, floor_rows):
-    product = jnp.dot(ordered, stacked, preferred_element_type=F32)
+    return finished(jnp.dot(ordered, stacked, preferred_element_type=F32), weights, first_row, floor_rows)
+
+
+def finished(product, weights, first_row, floor_rows):
     size = product.shape[0] // 2
     half = product.shape[1] // 2
     wr = weights[0:1, :half]
@@ -91,15 +93,18 @@
     ref[:, ref.shape[1] - 2 * BS :, :] = edge
 
 
+def chunk_sizes(blocks):
+    return [part * blocks // sum(CHUNKS) for part in CHUNKS]
+
+
 def load(
     main_hbm, side_hbm, field_hbm, coupling_hbm, floors_hbm,
     receivers_hbm, ordered_ref, start_ref, edge_ref, weight_ref, floor_ref, pick_ref,
     main_buf, side_buf, field_buf, planes, perm_ref, coupling_buf, floors_buf, receivers_buf, sems, small_sems,
 ):
     blocks = ordered_ref.shape[0]
-    per = blocks // CHUNKS
-    rows = per * BS
-    op_rows = rows * 6
+    sizes = chunk_sizes(blocks)
+    firsts = [sum(sizes[:n]) for n in range(len(sizes))]
     width = field_buf.shape[1]
     coupling_copy = pltpu.make_async_copy(coupling_hbm, coupling_buf, small_sems.at[0])
     floors_copy = pltpu.make_async_copy(floors_hbm, floors_buf, small_sems.at[1])
@@ -108,14 +113,14 @@
     floors_copy.start()
     receivers_copy.start()
     copies = []
-    for n in range(CHUNKS):
+    for n, (first, count) in enumerate(zip(firsts, sizes)):
         copies.append(
             [
                 pltpu.make_async_copy(
-                    source.at[pl.ds(n * size, size), :], buf.at[pl.ds(n * size, size), :], sems.at[kind, n]
+                    source.at[pl.ds(first * size, count * size), :], buf.at[pl.ds(first * size, count * size), :], sems.at[kind, n]
                 )
                 for kind, (source, buf, size) in enumerate(
-                    ((field_hbm, field_buf, rows), (main_hbm, main_buf, op_rows), (side_hbm, side_buf, op_rows))
+                    ((field_hbm, field_buf, BS), (main_hbm, main_buf, 6 * BS), (side_hbm, side_buf, 6 * BS))
                 )
             ]
         )
@@ -145,28 +150,26 @@
         pick_ref[...] = jnp.where(lax.axis_index("depth") == 0, turned, local)
 
     def split_chunk(n):
-        for j in range(per):
-            b = n * per + j
+        for b in range(firsts[n], firsts[n] + sizes[n]):
             field = jnp.dot(field_buf[b * BS : (b + 1) * BS, :], perm_ref[...], preferred_element_type=F32).astype(BF16)
             put_block(start_ref, b + 1, field)
 
-    def order_block(n, j, kind):
-        b = n * per + j
+    def order_block(b, kind):
         buf = (main_buf, side_buf)[kind]
-        plane = planes.at[(n % 2) * 2 * per + j * 2 + kind]
+        plane = planes.at[(b * 2 + kind) % planes.shape[0]]
         plane[...] = buf[b * BS * 6 : (b + 1) * BS * 6, :].astype(F32)
         for m in range(6):
             ordered_ref[b, m, kind * BS : (kind + 1) * BS, :] = plane[pl.ds(m, BS, stride=6), :].astype(BF16)
 
-    for n in range(CHUNKS):
+    for n in range(len(sizes)):
         for kind in range(3):
             copies[n][kind].wait()
-            if n + AHEAD < CHUNKS:
+            if n + AHEAD < len(sizes):
                 copies[n + AHEAD][kind].start()
         split_chunk(n)
-        for j in range(per):
-            order_block(n, j, 0)
-            order_block(n, j, 1)
+        for b in range(firsts[n], firsts[n] + sizes[n]):
+            order_block(b, 0)
+            order_block(b, 1)
         if n == 1:
             coupling_copy.wait()
             floors_copy.wait()
@@ -186,18 +189,29 @@
         else:
             zero_ends(next_ref)
 
-        def some(n, carry):
-            for j in range(UNROLL):
-                b = n * UNROLL + j
-                at = pl.multiple_of(b * BS, BS)
-                field = advanced(operator_rows(ordered_ref, b), three_blocks(field_ref, b), weights, at, floors)
-                if last:
-                    put_final(next_ref, at, field)
-                else:
-                    put_block(next_ref, b + 1, field)
-            return carry
-
-        lax.fori_loop(0, blocks // UNROLL, some, 0)
+        def put(b, product):
+            field = finished(product, weights, b * BS, floors)
+            if last:
+                put_final(next_ref, b * BS, field)
+            else:
+                put_block(next_ref, b + 1, field)
+
+        def rows_of(b, k):
+            return jnp.concatenate([ordered_ref[b, 2 * k], ordered_ref[b, 2 * k + 1]], axis=1)
+
+        opened, half_done = None, None
+        for b in range(blocks):
+            at = (b + 1) * 2 * BS
+            readers = [r for r in (b + 1, b, b - 1) if 0 <= r < blocks]
+            left = jnp.concatenate([rows_of(r, b - r + 1) for r in readers], axis=0)
+            right = jnp.concatenate([field_ref[0, at : at + 2 * BS, :], field_ref[1, at : at + 2 * BS, :]], axis=1)
+            product = jnp.dot(left, right, preferred_element_type=F32)
+            part = {r: product[i * 2 * BS : (i + 1) * 2 * BS] for i, r in enumerate(readers)}
+            if b > 0:
+                put(b - 1, half_done + part[b - 1])
+            half_done = part[b] if opened is None else opened + part[b]
+            opened = part.get(b + 1)
+        put(blocks - 1, half_done)
 
     return kernel
 
@@ -231,22 +245,31 @@
 
 def edge_and_pick(
     ordered_ref, field_ref, weight_ref, floor_ref, halo_ref, in_ref, rows_vmem,
-    final_ref, keep_ref, send_ref, halo_buf, picked, rows_ref, sem,
+    final_ref, send_ref, halo_buf, picked, rows_ref, sem,
 ):
     del in_ref
     rows_copy = pltpu.make_async_copy(rows_vmem, rows_ref, sem)
     rows_copy.start()
     b, field = edge_block(STEPS - 1, ordered_ref, field_ref, weight_ref, floor_ref, halo_ref, halo_buf)
     put_final(final_ref, pl.multiple_of(b * BS, BS), field)
-    owned = keep_ref.shape[0]
+    rows_copy.wait()
+    gather_rows(final_ref, rows_ref, 0, picked, send_ref)
+
+
+def pick_own(final_ref, rows_vmem, keep_ref, picked, rows_ref, sem):
+    rows_copy = pltpu.make_async_copy(rows_vmem, rows_ref, sem)
+    rows_copy.start()
+    rows_copy.wait()
+    gather_rows(final_ref, rows_ref, keep_ref.shape[0], picked, keep_ref)
+
+
+def gather_rows(final_ref, rows_ref, first, picked, out_ref):
     lanes = rows_ref.shape[1]
-    rows_copy.wait()
-    for which, out_ref in enumerate((send_ref, keep_ref)):
-        for n in range(owned):
-            at = rows_ref[(which * owned + n) // lanes, n % lanes]
-            for part in range(2):
-                picked[part, n : n + 1, :] = final_ref[part, pl.ds(at, 1), :]
-        out_ref[...] = jnp.concatenate([picked[0], picked[1]], axis=1).astype(BF16)
+    for n in range(out_ref.shape[0]):
+        at = rows_ref[(first + n) // lanes, (first + n) % lanes]
+        for part in range(2):
+            picked[part, n : n + 1, :] = final_ref[part, pl.ds(at, 1), :]
+    out_ref[...] = jnp.concatenate([picked[0], picked[1]], axis=1).astype(BF16)
 
 
 def basis_kernel(freq_ref, out_ref):
@@ -311,12 +334,12 @@
             pltpu.VMEM((rows * 6, BS), BF16),
             pltpu.VMEM((rows * 6, BS), BF16),
             pltpu.VMEM((rows, width), BF16),
-            pltpu.VMEM((4 * blocks // CHUNKS, BS * 6, BS), F32),
+            pltpu.VMEM((16, BS * 6, BS), F32),
             pltpu.VMEM((width, width), BF16),
             pltpu.VMEM((1, width), F32),
             pltpu.SMEM((STEPS,), jnp.int32),
             pltpu.VMEM((receivers.shape[0] // BS, BS), jnp.int32),
-            pltpu.SemaphoreType.DMA((3, CHUNKS)),
+            pltpu.SemaphoreType.DMA((3, len(CHUNKS))),
             pltpu.SemaphoreType.DMA((3,)),
         ],
         compiler_params=limit(28),
@@ -356,23 +379,32 @@
         )(ordered, before, weights, floor_rows, halo, field)
 
     owned = receivers.shape[0] // lax.axis_size("depth")
-    _, keep, send = pl.pallas_call(
+    pick_scratch = [
+        pltpu.VMEM((2, owned, width // 2), F32),
+        pltpu.SMEM(pick_rows.shape, jnp.int32),
+        pltpu.SemaphoreType.DMA,
+    ]
+    final, send = pl.pallas_call(
         edge_and_pick,
-        out_shape=(vmem((2, rows + 8, width // 2), F32), vmem((owned, width), BF16), vmem((owned, width), BF16)),
+        out_shape=(vmem((2, rows + 8, width // 2), F32), vmem((owned, width), BF16)),
         in_specs=[VMEM_SPEC] * 7,
-        out_specs=(VMEM_SPEC,) * 3,
+        out_specs=(VMEM_SPEC,) * 2,
         input_output_aliases={5: 0},
-        scratch_shapes=[
-            halo_buf,
-            pltpu.VMEM((2, owned, width // 2), F32),
-            pltpu.SMEM(pick_rows.shape, jnp.int32),
-            pltpu.SemaphoreType.DMA,
-        ],
+        scratch_shapes=[halo_buf] + pick_scratch,
         compiler_params=limit(6),
         name="edge_and_pick",
     )(ordered, before, weights, floor_rows, halo, field, pick_rows)
 
     got = lax.ppermute(send, "depth", swap)
+    keep = pl.pallas_call(
+        pick_own,
+        out_shape=vmem((owned, width), BF16),
+        in_specs=[VMEM_SPEC] * 2,
+        out_specs=VMEM_SPEC,
+        scratch_shapes=pick_scratch,
+        compiler_params=limit(6),
+        name="pick_own",
+    )(final, pick_rows)
     keep2 = lax.ppermute(keep, "core", swap)
     basis = pl.pallas_call(
         basis_kernel,

time: 60.2 us -> 59.6 us (0.990)
  waiting for transfers between devices: 4.51 us -> 3.65 us
    ppermute x1, waiting for transfers between devices: 3.65 us -> 2.79 us  [local(): got = lax.ppermute(send, 'depth', swap)]
    pallas_call x0 -> x1, Pallas kernels: none -> 0.85 us  [local(): pl.pallas_call(pick_own, out_shape=vmem((owned, width), BF16), in_specs=[...]
  transfers between devices with their start and end apart: 7 -> 7, of which waited for: 2 -> 2; matrix products, arithmetic and copies ran while one was open for 0% -> 0% of each run, Pallas kernels for 25% -> 26%
where the time goes in v4:
time: 59.6 us; the launch traced here: 59.5 us
  Pallas kernels  24.3 us (41%)
  blocking collectives  24 us (40%)
  starting transfers between devices  6.73 us (11%)
  waiting for transfers between devices  3.65 us (6%)
  other arithmetic  0.7 us (1%)
    all_to_all x1, blocking collectives, local(): lax.all_to_all(partial.reshape(groups, NT // 2 // groups, owned), others,...  24 us
    pallas_call x4, Pallas kernels, local(): pl.pallas_call(whole_step(step, last), out_shape=vmem((2, rows + 8, width...  13.8 us
    pallas_call x1, Pallas kernels, local(): pl.pallas_call(load, out_shape=(vmem((blocks, 6, 2 * BS, BS), BF16), vmem...  6.72 us
    ppermute x4, starting transfers between devices, local(): halo = lax.ppermute(edge, 'depth', swap)  5.34 us
    ppermute x1, waiting for transfers between devices, local(): got = lax.ppermute(send, 'depth', swap)  2.79 us
    ppermute x1, starting transfers between devices, local(): got = lax.ppermute(send, 'depth', swap)  1.3 us
  transfers between devices with their start and end apart: 7, of which 2 were waited for; matrix products, arithmetic and copies ran while one was open for 0% of the time, Pallas kernels for 26%

profile of v4, /device:TPU:0, one launch (start us, length us, event | category | flops | bytes accessed | tf_op | source)
XLA Modules:
  0.0 59.5 jit_solution(13925797634452830762)
XLA Ops:
  0.0 6.7 %load.1 = (bf16[32,6,256,128]{3,2,1,0:T(8,128)(2,1)S(1)}, bf16[2,8704,128]{2,1,0:T(8,128)(2,1)S(1)}, bf16[128,256]{1,0:T(8,128)(2,1)S(1)}, f32[8,256]{1,0:T(8,12...) custom-call(bf16[24576,128]{1,0:T(8,128)(2,1)} %bitcast.10, bf16[24576,128]{1,0:T(8,128)(2,1)} %bitcast.11, ...), custom_call_target="tpu_custom_call" | custom-call | tf_op jit(solution)/shard_map/load/pallas_call | solution.py:321
  6.7 2.1 %collective-permute-start = (bf16[128,256]{1,0:T(8,128)(2,1)S(1)}, bf16[128,256]{1,0:T(8,128)(2,1)S(1)}, u32[]{:S(2)}, u32[]{:S(2)}) collective-permute-start(bf16[128,256]{1,0:T(8,128)(2,1)S(1)} %get-tuple-element.23), channel_id=1, source_target_pairs={{0,1},{1,0},{2,3},{3,2},{4,5},{5,4},{6,7},{7,6},{8,9},{9,8},{10,11... | collective-permute-start | bytes 196616 | tf_op jit(solution)/shard_map/ppermute | solution.py:359
  8.8 3.4 %whole_step.4.in_ref = bf16[2,8704,128]{2,1,0:T(8,128)(2,1)S(1)} custom-call(bf16[32,6,256,128]{3,2,1,0:T(8,128)(2,1)S(1)} %get-tuple-element.19.ordered_ref, bf16[2,8704,128]{2,1,0:T(8,128)(2,1)S(1)} %get-tuple-element.20.field_ref, f32[8,256]{1,0:T(8,128)S(1)} %get-tuple-element.21.weight_ref, s32[8,128]{1,0:T(8,128)S(1)} %get-tuple-element.22.floor_ref), custom_call_target="tpu_custom_call" | custom-call | tf_op jit(solution)/shard_map/whole_step/pallas_call | solution.py:360
  12.3 0.0 collective-permute-done.halo_ref
  12.3 0.3 edge_step.3
  12.6 0.9 %collective-permute-start.1 = (bf16[128,256]{1,0:T(8,128)(2,1)S(1)}, bf16[128,256]{1,0:T(8,128)(2,1)S(1)}, u32[]{:S(2)}, u32[]{:S(2)}) collective-permute-start(bf16[128,256]{1,0:T(8,128)(2,1)S(1)} %get-tuple-element.25), channel_id=1, source_target_pairs={{0,1},{1,0},{2,3},{3,2},{4,5},{5,4},{6,7},{7,6},{8,9},{9,8},{10,11... | collective-permute-start | bytes 196616 | tf_op jit(solution)/shard_map/ppermute | solution.py:359
  13.5 3.4 %whole_step.5.in_ref = bf16[2,8704,128]{2,1,0:T(8,128)(2,1)S(1)} custom-call(bf16[32,6,256,128]{3,2,1,0:T(8,128)(2,1)S(1)} %get-tuple-element.19.ordered_ref, bf16[2,8704,128]{2,1,0:T(8,128)(2,1)S(1)} %get-tuple-element.24.field_ref, f32[8,256]{1,0:T(8,128)S(1)} %get-tuple-element.21.weight_ref, s32[8,128]{1,0:T(8,128)S(1)} %get-tuple-element.22.floor_ref), custom_call_target="tpu_custom_call" | custom-call | tf_op jit(solution)/shard_map/whole_step/pallas_call | solution.py:360
  16.9 0.0 collective-permute-done.1.halo_ref
  17.0 0.3 edge_step.4
  17.3 1.5 %collective-permute-start.2 = (bf16[128,256]{1,0:T(8,128)(2,1)S(1)}, bf16[128,256]{1,0:T(8,128)(2,1)S(1)}, u32[]{:S(2)}, u32[]{:S(2)}) collective-permute-start(bf16[128,256]{1,0:T(8,128)(2,1)S(1)} %get-tuple-element.27), channel_id=1, source_target_pairs={{0,1},{1,0},{2,3},{3,2},{4,5},{5,4},{6,7},{7,6},{8,9},{9,8},{10,11... | collective-permute-start | bytes 196616 | tf_op jit(solution)/shard_map/ppermute | solution.py:359
  18.8 3.5 %whole_step.6.in_ref = bf16[2,8704,128]{2,1,0:T(8,128)(2,1)S(1)} custom-call(bf16[32,6,256,128]{3,2,1,0:T(8,128)(2,1)S(1)} %get-tuple-element.19.ordered_ref, bf16[2,8704,128]{2,1,0:T(8,128)(2,1)S(1)} %get-tuple-element.26.field_ref, f32[8,256]{1,0:T(8,128)S(1)} %get-tuple-element.21.weight_ref, s32[8,128]{1,0:T(8,128)S(1)} %get-tuple-element.22.floor_ref), custom_call_target="tpu_custom_call" | custom-call | tf_op jit(solution)/shard_map/whole_step/pallas_call | solution.py:360
  22.3 0.0 collective-permute-done.2.halo_ref
  22.3 0.3 edge_step.5
  22.6 0.9 %collective-permute-start.3 = (bf16[128,256]{1,0:T(8,128)(2,1)S(1)}, bf16[128,256]{1,0:T(8,128)(2,1)S(1)}, u32[]{:S(2)}, u32[]{:S(2)}) collective-permute-start(bf16[128,256]{1,0:T(8,128)(2,1)S(1)} %get-tuple-element.29), channel_id=1, source_target_pairs={{0,1},{1,0},{2,3},{3,2},{4,5},{5,4},{6,7},{7,6},{8,9},{9,8},{10,11... | collective-permute-start | bytes 196616 | tf_op jit(solution)/shard_map/ppermute | solution.py:359
  23.5 3.4 %whole_step.7.in_ref = f32[2,4104,128]{2,1,0:T(8,128)S(1)} custom-call(bf16[32,6,256,128]{3,2,1,0:T(8,128)(2,1)S(1)} %get-tuple-element.19.ordered_ref, bf16[2,8704,128]{2,1,0:T(8,128)(2,1)S(1)} %get-tuple-element.28.field_ref, f32[8,256]{1,0:T(8,128)S(1)} %get-tuple-element.21.weight_ref, s32[8,128]{1,0:T(8,128)S(1)} %get-tuple-element.22.floor_ref), custom_call_target="tpu_custom_call" | custom-call | tf_op jit(solution)/shard_map/whole_step/pallas_call | solution.py:360
  26.9 0.0 collective-permute-done.3.halo_ref
  27.0 0.0 copy-start
  27.0 0.9 %edge_and_pick.1 = (f32[2,4104,128]{2,1,0:T(8,128)S(1)}, bf16[256,256]{1,0:T(8,128)(2,1)S(1)}) custom-call(bf16[32,6,256,128]{3,2,1,0:T(8,128)(2,1)S(1)} %get-tuple-element.19.ordered_ref, bf16[2,8704,128]{2,1,0:T(8,128)(2,1)S(1)} %get-tuple-element.28.field_ref, f32[8,256]{1,0:T(8,128)S(1)} %get-tuple-element.21.weight_ref, ...), custom_call_target="tpu_custom_call", output_to_operand_aliasing={{0}: (5, {})} | custom-call | tf_op jit(solution)/shard_map/edge_and_pick/pallas_call | solution.py:387
  27.9 1.3 %collective-permute-start.4 = (bf16[256,256]{1,0:T(8,128)(2,1)S(1)}, bf16[256,256]{1,0:T(8,128)(2,1)S(1)}, u32[]{:S(2)}, u32[]{:S(2)}) collective-permute-start(bf16[256,256]{1,0:T(8,128)(2,1)S(1)} %get-tuple-element.32), channel_id=1, source_target_pairs={{0,1},{1,0},{2,3},{3,2},{4,5},{5,4},{6,7},{7,6},{8,9},{9,8},{10,11... | collective-permute-start | bytes 393224 | tf_op jit(solution)/shard_map/ppermute | solution.py:398
  29.2 0.9 %pick_own.1.keep_ref = bf16[256,256]{1,0:T(8,128)(2,1)S(1)} custom-call(f32[2,4104,128]{2,1,0:T(8,128)S(1)} %get-tuple-element.31.final_ref, s32[4,128]{1,0:T(4,128)S(1)} %get-tuple-element.30.rows_vmem), custom_call_target="tpu_custom_call" | custom-call | tf_op jit(solution)/shard_map/pick_own/pallas_call | solution.py:399
  30.1 0.1 collective-permute-start.5
  30.2 2.8 %collective-permute-done.4.got_ref = bf16[256,256]{1,0:T(8,128)(2,1)S(1)} collective-permute-done((bf16[256,256]{1,0:T(8,128)(2,1)S(1)}, bf16[256,256]{1,0:T(8,128)(2,1)S(1)}, u32[]{:S(2)}, u32[]{:S(2)}) %collective-permute-start.4) | collective-permute-done | bytes 131104 | tf_op jit(solution)/shard_map/ppermute | solution.py:398
  33.0 0.0 collective-permute-start.6
  33.0 0.0 copy-done
  33.0 0.5 basis.1.basis_ref
  33.5 0.0 collective-permute-done.5.keep2_ref
  33.5 0.8 %collective-permute-done.6.got2_ref = bf16[256,256]{1,0:T(8,128)(2,1)S(1)} collective-permute-done((bf16[256,256]{1,0:T(8,128)(2,1)S(1)}, bf16[256,256]{1,0:T(8,128)(2,1)S(1)}, u32[]{:S(2)}, u32[]{:S(2)}) %collective-permute-start.6) | collective-permute-done | bytes 131104 | tf_op jit(solution)/shard_map/ppermute | solution.py:417
  34.3 0.5 series.1
  34.8 24.0 %all_to_all.5 = bf16[32,32,256]{2,1,0:T(8,128)(2,1)S(1)} all-to-all(bf16[32,32,256]{2,1,0:T(8,128)(2,1)S(1)} %bitcast.8), channel_id=1, replica_groups=mesh['x'=4,'y'=4,'zh'=2,'core'=2,'depth'=2] {'x','y','zh'}, dimensions={0} | all-to-all | bytes 1048576 | tf_op jit(solution)/shard_map/all_to_all | solution.py:428
  58.8 0.1 convert_reduce_fusion
  58.9 0.6 %multiply_bitcast_fusion = f32[256,32]{0,1:T(8,128)} fusion(f32[32,256]{1,0:T(8,128)S(1)} %convert_reduce_fusion), kind=kLoop, calls=%fused_computation.1 | loop fusion | flops 8192 | bytes 65536 | tf_op jit(solution)/shard_map/mul | solution.py:431
Async XLA Ops:
  6.7 5.5 %collective-permute-start = (bf16[128,256]{1,0:T(8,128)(2,1)S(1)}, bf16[128,256]{1,0:T(8,128)(2,1)S(1)}, u32[]{:S(2)}, u32[]{:S(2)}) collective-permute-start(bf16[128,256]{1,0:T(8,128)(2,1)S(1)} %get-tuple-element.23), channel_id=1, source_target_pairs={{0,1},{1,0},{2,3},{3,2},{4,5},{5,4},{6,7},{7,6},{8,9},{9,8},{10,11... | collective-permute-start | bytes 196616 | tf_op jit(solution)/shard_map/ppermute | solution.py:359
  12.6 4.3 %collective-permute-start.1 = (bf16[128,256]{1,0:T(8,128)(2,1)S(1)}, bf16[128,256]{1,0:T(8,128)(2,1)S(1)}, u32[]{:S(2)}, u32[]{:S(2)}) collective-permute-start(bf16[128,256]{1,0:T(8,128)(2,1)S(1)} %get-tuple-element.25), channel_id=1, source_target_pairs={{0,1},{1,0},{2,3},{3,2},{4,5},{5,4},{6,7},{7,6},{8,9},{9,8},{10,11... | collective-permute-start | bytes 196616 | tf_op jit(solution)/shard_map/ppermute | solution.py:359
  17.3 5.0 %collective-permute-start.2 = (bf16[128,256]{1,0:T(8,128)(2,1)S(1)}, bf16[128,256]{1,0:T(8,128)(2,1)S(1)}, u32[]{:S(2)}, u32[]{:S(2)}) collective-permute-start(bf16[128,256]{1,0:T(8,128)(2,1)S(1)} %get-tuple-element.27), channel_id=1, source_target_pairs={{0,1},{1,0},{2,3},{3,2},{4,5},{5,4},{6,7},{7,6},{8,9},{9,8},{10,11... | collective-permute-start | bytes 196616 | tf_op jit(solution)/shard_map/ppermute | solution.py:359
  22.6 4.3 %collective-permute-start.3 = (bf16[128,256]{1,0:T(8,128)(2,1)S(1)}, bf16[128,256]{1,0:T(8,128)(2,1)S(1)}, u32[]{:S(2)}, u32[]{:S(2)}) collective-permute-start(bf16[128,256]{1,0:T(8,128)(2,1)S(1)} %get-tuple-element.29), channel_id=1, source_target_pairs={{0,1},{1,0},{2,3},{3,2},{4,5},{5,4},{6,7},{7,6},{8,9},{9,8},{10,11... | collective-permute-start | bytes 196616 | tf_op jit(solution)/shard_map/ppermute | solution.py:359
  27.0 6.0 %copy-start = (f32[8192]{0:T(1024)S(1)}, f32[8192]{0:T(1024)}, u32[]{:S(2)}) copy-start(f32[8192]{0:T(1024)} %param.11) | copy-start | bytes 98308
  27.9 5.0 %collective-permute-start.4 = (bf16[256,256]{1,0:T(8,128)(2,1)S(1)}, bf16[256,256]{1,0:T(8,128)(2,1)S(1)}, u32[]{:S(2)}, u32[]{:S(2)}) collective-permute-start(bf16[256,256]{1,0:T(8,128)(2,1)S(1)} %get-tuple-element.32), channel_id=1, source_target_pairs={{0,1},{1,0},{2,3},{3,2},{4,5},{5,4},{6,7},{7,6},{8,9},{9,8},{10,11... | collective-permute-start | bytes 393224 | tf_op jit(solution)/shard_map/ppermute | solution.py:398
  30.1 3.4 %collective-permute-start.5 = (bf16[256,256]{1,0:T(8,128)(2,1)S(1)}, bf16[256,256]{1,0:T(8,128)(2,1)S(1)}, u32[]{:S(2)}, u32[]{:S(2)}) collective-permute-start(bf16[256,256]{1,0:T(8,128)(2,1)S(1)} %pick_own.1.keep_ref), channel_id=1, source_target_pairs={{0,2},{2,0},{1,3},{3,1},{4,6},{6,4},{5,7},{7,5},{8,10},{10,8},{9,1... | collective-permute-start | bytes 393224 | tf_op jit(solution)/shard_map/ppermute | solution.py:408
  33.0 1.3 %collective-permute-start.6 = (bf16[256,256]{1,0:T(8,128)(2,1)S(1)}, bf16[256,256]{1,0:T(8,128)(2,1)S(1)}, u32[]{:S(2)}, u32[]{:S(2)}) collective-permute-start(bf16[256,256]{1,0:T(8,128)(2,1)S(1)} %collective-permute-done.4.got_ref), channel_id=1, source_target_pairs={{0,2},{2,0},{1,3},{3,1},{4,6},{6,4},{5,7},{7,5},{8,10},{10,8},{9,1... | collective-permute-start | bytes 393224 | tf_op jit(solution)/shard_map/ppermute | solution.py:417

commit v5 on v4

--- a/solution.py
+++ b/solution.py
@@ -1,3 +1,4 @@
+import functools
 import math
 
 import jax
@@ -306,10 +307,10 @@
     lax.fori_loop(0, NT // (2 * spread), some, tuple(state))
 
 
-def series_kernel(basis_ref, keep_ref, got_ref, keep2_ref, got2_ref, out_ref):
+def series_kernel(factor, basis_ref, keep_ref, got_ref, keep2_ref, got2_ref, out_ref):
     picked = jnp.concatenate([keep_ref[...] + got_ref[...], keep2_ref[...] + got2_ref[...]], axis=1)
     product = lax.dot_general(basis_ref[...], picked, (((1,), (1,)), ((), ())), preferred_element_type=F32)
-    out_ref[...] = product.astype(BF16)
+    out_ref[...] = (product * factor).astype(BF16)
 
 
 def local(pressure_field, block_main, block_coupled, coupling, frequencies, receivers, floors):
@@ -416,7 +417,7 @@
     )(frequencies.reshape(-1, width // 2))
     got2 = lax.ppermute(got, "core", swap)
     partial = pl.pallas_call(
-        series_kernel,
+        functools.partial(series_kernel, 1.0 / math.sqrt(frequencies.shape[0])),
         out_shape=jax.ShapeDtypeStruct((NT // 2, owned), BF16),
         in_specs=[VMEM_SPEC] * 5,
         out_specs=VMEM_SPEC,
@@ -428,8 +429,7 @@
     arrived = lax.all_to_all(
         partial.reshape(groups, NT // 2 // groups, owned), others, split_axis=0, concat_axis=0, tiled=True
     )
-    summed = arrived.astype(F32).sum(axis=0) * (1.0 / math.sqrt(frequencies.shape[0]))
-    return summed.T
+    return arrived.astype(F32).sum(axis=0).T
 
 
 def solution(mesh):

time: 59.6 us -> 59.6 us (level)
    mul x1 -> x0, other arithmetic: 0.62 us -> none  [local(): arrived.astype(F32).sum(axis=0) * (1.0 / math.sqrt(frequencies.shape[0]))]
    reduce_sum x1, other arithmetic: 0.08 us -> 0.7 us  [local(): return arrived.astype(F32).sum(axis=0).T]
where the time goes in v5:
time: 59.6 us; the launch traced here: 59.5 us
  Pallas kernels  24.3 us (41%)
  blocking collectives  24 us (40%)
  starting transfers between devices  6.73 us (11%)
  waiting for transfers between devices  3.65 us (6%)
  other arithmetic  0.7 us (1%)
    all_to_all x1, blocking collectives, local(): lax.all_to_all(partial.reshape(groups, NT // 2 // groups, owned), others,...  24 us
    pallas_call x4, Pallas kernels, local(): pl.pallas_call(whole_step(step, last), out_shape=vmem((2, rows + 8, width...  13.8 us
    pallas_call x1, Pallas kernels, local(): pl.pallas_call(load, out_shape=(vmem((blocks, 6, 2 * BS, BS), BF16), vmem...  6.72 us
    ppermute x4, starting transfers between devices, local(): halo = lax.ppermute(edge, 'depth', swap)  5.34 us
    ppermute x1, waiting for transfers between devices, local(): got = lax.ppermute(send, 'depth', swap)  2.79 us
    ppermute x1, starting transfers between devices, local(): got = lax.ppermute(send, 'depth', swap)  1.3 us
  transfers between devices with their start and end apart: 7, of which 2 were waited for; matrix products, arithmetic and copies ran while one was open for 0% of the time, Pallas kernels for 26%

profile of v5, /device:TPU:0, one launch (start us, length us, event | category | flops | bytes accessed | tf_op | source)
XLA Modules:
  0.0 59.5 jit_solution(1870128973959399867)
XLA Ops:
  0.0 6.7 %load.1 = (bf16[32,6,256,128]{3,2,1,0:T(8,128)(2,1)S(1)}, bf16[2,8704,128]{2,1,0:T(8,128)(2,1)S(1)}, bf16[128,256]{1,0:T(8,128)(2,1)S(1)}, f32[8,256]{1,0:T(8,12...) custom-call(bf16[24576,128]{1,0:T(8,128)(2,1)} %bitcast.9, bf16[24576,128]{1,0:T(8,128)(2,1)} %bitcast.10, ...), custom_call_target="tpu_custom_call" | custom-call | tf_op jit(solution)/shard_map/load/pallas_call | solution.py:322
  6.7 2.1 %collective-permute-start = (bf16[128,256]{1,0:T(8,128)(2,1)S(1)}, bf16[128,256]{1,0:T(8,128)(2,1)S(1)}, u32[]{:S(2)}, u32[]{:S(2)}) collective-permute-start(bf16[128,256]{1,0:T(8,128)(2,1)S(1)} %get-tuple-element.23), channel_id=1, source_target_pairs={{0,1},{1,0},{2,3},{3,2},{4,5},{5,4},{6,7},{7,6},{8,9},{9,8},{10,11... | collective-permute-start | bytes 196616 | tf_op jit(solution)/shard_map/ppermute | solution.py:360
  8.8 3.4 %whole_step.4.in_ref = bf16[2,8704,128]{2,1,0:T(8,128)(2,1)S(1)} custom-call(bf16[32,6,256,128]{3,2,1,0:T(8,128)(2,1)S(1)} %get-tuple-element.19.ordered_ref, bf16[2,8704,128]{2,1,0:T(8,128)(2,1)S(1)} %get-tuple-element.20.field_ref, f32[8,256]{1,0:T(8,128)S(1)} %get-tuple-element.21.weight_ref, s32[8,128]{1,0:T(8,128)S(1)} %get-tuple-element.22.floor_ref), custom_call_target="tpu_custom_call" | custom-call | tf_op jit(solution)/shard_map/whole_step/pallas_call | solution.py:361
  12.3 0.0 collective-permute-done.halo_ref
  12.3 0.3 edge_step.3
  12.6 0.9 %collective-permute-start.1 = (bf16[128,256]{1,0:T(8,128)(2,1)S(1)}, bf16[128,256]{1,0:T(8,128)(2,1)S(1)}, u32[]{:S(2)}, u32[]{:S(2)}) collective-permute-start(bf16[128,256]{1,0:T(8,128)(2,1)S(1)} %get-tuple-element.25), channel_id=1, source_target_pairs={{0,1},{1,0},{2,3},{3,2},{4,5},{5,4},{6,7},{7,6},{8,9},{9,8},{10,11... | collective-permute-start | bytes 196616 | tf_op jit(solution)/shard_map/ppermute | solution.py:360
  13.5 3.4 %whole_step.5.in_ref = bf16[2,8704,128]{2,1,0:T(8,128)(2,1)S(1)} custom-call(bf16[32,6,256,128]{3,2,1,0:T(8,128)(2,1)S(1)} %get-tuple-element.19.ordered_ref, bf16[2,8704,128]{2,1,0:T(8,128)(2,1)S(1)} %get-tuple-element.24.field_ref, f32[8,256]{1,0:T(8,128)S(1)} %get-tuple-element.21.weight_ref, s32[8,128]{1,0:T(8,128)S(1)} %get-tuple-element.22.floor_ref), custom_call_target="tpu_custom_call" | custom-call | tf_op jit(solution)/shard_map/whole_step/pallas_call | solution.py:361
  16.9 0.0 collective-permute-done.1.halo_ref
  17.0 0.3 edge_step.4
  17.3 1.5 %collective-permute-start.2 = (bf16[128,256]{1,0:T(8,128)(2,1)S(1)}, bf16[128,256]{1,0:T(8,128)(2,1)S(1)}, u32[]{:S(2)}, u32[]{:S(2)}) collective-permute-start(bf16[128,256]{1,0:T(8,128)(2,1)S(1)} %get-tuple-element.27), channel_id=1, source_target_pairs={{0,1},{1,0},{2,3},{3,2},{4,5},{5,4},{6,7},{7,6},{8,9},{9,8},{10,11... | collective-permute-start | bytes 196616 | tf_op jit(solution)/shard_map/ppermute | solution.py:360
  18.8 3.5 %whole_step.6.in_ref = bf16[2,8704,128]{2,1,0:T(8,128)(2,1)S(1)} custom-call(bf16[32,6,256,128]{3,2,1,0:T(8,128)(2,1)S(1)} %get-tuple-element.19.ordered_ref, bf16[2,8704,128]{2,1,0:T(8,128)(2,1)S(1)} %get-tuple-element.26.field_ref, f32[8,256]{1,0:T(8,128)S(1)} %get-tuple-element.21.weight_ref, s32[8,128]{1,0:T(8,128)S(1)} %get-tuple-element.22.floor_ref), custom_call_target="tpu_custom_call" | custom-call | tf_op jit(solution)/shard_map/whole_step/pallas_call | solution.py:361
  22.3 0.0 collective-permute-done.2.halo_ref
  22.3 0.3 edge_step.5
  22.6 0.9 %collective-permute-start.3 = (bf16[128,256]{1,0:T(8,128)(2,1)S(1)}, bf16[128,256]{1,0:T(8,128)(2,1)S(1)}, u32[]{:S(2)}, u32[]{:S(2)}) collective-permute-start(bf16[128,256]{1,0:T(8,128)(2,1)S(1)} %get-tuple-element.29), channel_id=1, source_target_pairs={{0,1},{1,0},{2,3},{3,2},{4,5},{5,4},{6,7},{7,6},{8,9},{9,8},{10,11... | collective-permute-start | bytes 196616 | tf_op jit(solution)/shard_map/ppermute | solution.py:360
  23.5 3.4 %whole_step.7.in_ref = f32[2,4104,128]{2,1,0:T(8,128)S(1)} custom-call(bf16[32,6,256,128]{3,2,1,0:T(8,128)(2,1)S(1)} %get-tuple-element.19.ordered_ref, bf16[2,8704,128]{2,1,0:T(8,128)(2,1)S(1)} %get-tuple-element.28.field_ref, f32[8,256]{1,0:T(8,128)S(1)} %get-tuple-element.21.weight_ref, s32[8,128]{1,0:T(8,128)S(1)} %get-tuple-element.22.floor_ref), custom_call_target="tpu_custom_call" | custom-call | tf_op jit(solution)/shard_map/whole_step/pallas_call | solution.py:361
  26.9 0.0 collective-permute-done.3.halo_ref
  27.0 0.0 copy-start
  27.0 0.9 %edge_and_pick.1 = (f32[2,4104,128]{2,1,0:T(8,128)S(1)}, bf16[256,256]{1,0:T(8,128)(2,1)S(1)}) custom-call(bf16[32,6,256,128]{3,2,1,0:T(8,128)(2,1)S(1)} %get-tuple-element.19.ordered_ref, bf16[2,8704,128]{2,1,0:T(8,128)(2,1)S(1)} %get-tuple-element.28.field_ref, f32[8,256]{1,0:T(8,128)S(1)} %get-tuple-element.21.weight_ref, ...), custom_call_target="tpu_custom_call", output_to_operand_aliasing={{0}: (5, {})} | custom-call | tf_op jit(solution)/shard_map/edge_and_pick/pallas_call | solution.py:388
  27.9 1.3 %collective-permute-start.4 = (bf16[256,256]{1,0:T(8,128)(2,1)S(1)}, bf16[256,256]{1,0:T(8,128)(2,1)S(1)}, u32[]{:S(2)}, u32[]{:S(2)}) collective-permute-start(bf16[256,256]{1,0:T(8,128)(2,1)S(1)} %get-tuple-element.32), channel_id=1, source_target_pairs={{0,1},{1,0},{2,3},{3,2},{4,5},{5,4},{6,7},{7,6},{8,9},{9,8},{10,11... | collective-permute-start | bytes 393224 | tf_op jit(solution)/shard_map/ppermute | solution.py:399
  29.2 0.9 %pick_own.1.keep_ref = bf16[256,256]{1,0:T(8,128)(2,1)S(1)} custom-call(f32[2,4104,128]{2,1,0:T(8,128)S(1)} %get-tuple-element.31.final_ref, s32[4,128]{1,0:T(4,128)S(1)} %get-tuple-element.30.rows_vmem), custom_call_target="tpu_custom_call" | custom-call | tf_op jit(solution)/shard_map/pick_own/pallas_call | solution.py:400
  30.1 0.1 collective-permute-start.5
  30.2 2.8 %collective-permute-done.4.got_ref = bf16[256,256]{1,0:T(8,128)(2,1)S(1)} collective-permute-done((bf16[256,256]{1,0:T(8,128)(2,1)S(1)}, bf16[256,256]{1,0:T(8,128)(2,1)S(1)}, u32[]{:S(2)}, u32[]{:S(2)}) %collective-permute-start.4) | collective-permute-done | bytes 131104 | tf_op jit(solution)/shard_map/ppermute | solution.py:399
  33.0 0.0 collective-permute-start.6
  33.0 0.0 copy-done
  33.0 0.5 basis.1.basis_ref
  33.5 0.0 collective-permute-done.5.keep2_ref
  33.5 0.8 %collective-permute-done.6.got2_ref = bf16[256,256]{1,0:T(8,128)(2,1)S(1)} collective-permute-done((bf16[256,256]{1,0:T(8,128)(2,1)S(1)}, bf16[256,256]{1,0:T(8,128)(2,1)S(1)}, u32[]{:S(2)}, u32[]{:S(2)}) %collective-permute-start.6) | collective-permute-done | bytes 131104 | tf_op jit(solution)/shard_map/ppermute | solution.py:418
  34.3 0.5 series.1
  34.8 24.0 %all_to_all.5 = bf16[32,32,256]{2,1,0:T(8,128)(2,1)S(1)} all-to-all(bf16[32,32,256]{2,1,0:T(8,128)(2,1)S(1)} %bitcast.7), channel_id=1, replica_groups=mesh['x'=4,'y'=4,'zh'=2,'core'=2,'depth'=2] {'x','y','zh'}, dimensions={0} | all-to-all | bytes 1048576 | tf_op jit(solution)/shard_map/all_to_all | solution.py:429
  58.8 0.7 %convert_reduce_fusion = f32[32,256]{1,0:T(8,128)} fusion(bf16[32,32,256]{2,1,0:T(8,128)(2,1)S(1)} %all_to_all.5), kind=kLoop, calls=%fused_computation | loop fusion | flops 516096 | bytes 557056 | tf_op jit(solution)/shard_map/reduce_sum | solution.py:432
Async XLA Ops:
  6.7 5.5 %collective-permute-start = (bf16[128,256]{1,0:T(8,128)(2,1)S(1)}, bf16[128,256]{1,0:T(8,128)(2,1)S(1)}, u32[]{:S(2)}, u32[]{:S(2)}) collective-permute-start(bf16[128,256]{1,0:T(8,128)(2,1)S(1)} %get-tuple-element.23), channel_id=1, source_target_pairs={{0,1},{1,0},{2,3},{3,2},{4,5},{5,4},{6,7},{7,6},{8,9},{9,8},{10,11... | collective-permute-start | bytes 196616 | tf_op jit(solution)/shard_map/ppermute | solution.py:360
  12.6 4.3 %collective-permute-start.1 = (bf16[128,256]{1,0:T(8,128)(2,1)S(1)}, bf16[128,256]{1,0:T(8,128)(2,1)S(1)}, u32[]{:S(2)}, u32[]{:S(2)}) collective-permute-start(bf16[128,256]{1,0:T(8,128)(2,1)S(1)} %get-tuple-element.25), channel_id=1, source_target_pairs={{0,1},{1,0},{2,3},{3,2},{4,5},{5,4},{6,7},{7,6},{8,9},{9,8},{10,11... | collective-permute-start | bytes 196616 | tf_op jit(solution)/shard_map/ppermute | solution.py:360
  17.3 5.0 %collective-permute-start.2 = (bf16[128,256]{1,0:T(8,128)(2,1)S(1)}, bf16[128,256]{1,0:T(8,128)(2,1)S(1)}, u32[]{:S(2)}, u32[]{:S(2)}) collective-permute-start(bf16[128,256]{1,0:T(8,128)(2,1)S(1)} %get-tuple-element.27), channel_id=1, source_target_pairs={{0,1},{1,0},{2,3},{3,2},{4,5},{5,4},{6,7},{7,6},{8,9},{9,8},{10,11... | collective-permute-start | bytes 196616 | tf_op jit(solution)/shard_map/ppermute | solution.py:360
  22.6 4.3 %collective-permute-start.3 = (bf16[128,256]{1,0:T(8,128)(2,1)S(1)}, bf16[128,256]{1,0:T(8,128)(2,1)S(1)}, u32[]{:S(2)}, u32[]{:S(2)}) collective-permute-start(bf16[128,256]{1,0:T(8,128)(2,1)S(1)} %get-tuple-element.29), channel_id=1, source_target_pairs={{0,1},{1,0},{2,3},{3,2},{4,5},{5,4},{6,7},{7,6},{8,9},{9,8},{10,11... | collective-permute-start | bytes 196616 | tf_op jit(solution)/shard_map/ppermute | solution.py:360
  27.0 6.0 %copy-start = (f32[8192]{0:T(1024)S(1)}, f32[8192]{0:T(1024)}, u32[]{:S(2)}) copy-start(f32[8192]{0:T(1024)} %param.11) | copy-start | bytes 98308
  27.9 5.0 %collective-permute-start.4 = (bf16[256,256]{1,0:T(8,128)(2,1)S(1)}, bf16[256,256]{1,0:T(8,128)(2,1)S(1)}, u32[]{:S(2)}, u32[]{:S(2)}) collective-permute-start(bf16[256,256]{1,0:T(8,128)(2,1)S(1)} %get-tuple-element.32), channel_id=1, source_target_pairs={{0,1},{1,0},{2,3},{3,2},{4,5},{5,4},{6,7},{7,6},{8,9},{9,8},{10,11... | collective-permute-start | bytes 393224 | tf_op jit(solution)/shard_map/ppermute | solution.py:399
  30.1 3.4 %collective-permute-start.5 = (bf16[256,256]{1,0:T(8,128)(2,1)S(1)}, bf16[256,256]{1,0:T(8,128)(2,1)S(1)}, u32[]{:S(2)}, u32[]{:S(2)}) collective-permute-start(bf16[256,256]{1,0:T(8,128)(2,1)S(1)} %pick_own.1.keep_ref), channel_id=1, source_target_pairs={{0,2},{2,0},{1,3},{3,1},{4,6},{6,4},{5,7},{7,5},{8,10},{10,8},{9,1... | collective-permute-start | bytes 393224 | tf_op jit(solution)/shard_map/ppermute | solution.py:409
  33.0 1.3 %collective-permute-start.6 = (bf16[256,256]{1,0:T(8,128)(2,1)S(1)}, bf16[256,256]{1,0:T(8,128)(2,1)S(1)}, u32[]{:S(2)}, u32[]{:S(2)}) collective-permute-start(bf16[256,256]{1,0:T(8,128)(2,1)S(1)} %collective-permute-done.4.got_ref), channel_id=1, source_target_pairs={{0,2},{2,0},{1,3},{3,1},{4,6},{6,4},{5,7},{7,5},{8,10},{10,8},{9,1... | collective-permute-start | bytes 393224 | tf_op jit(solution)/shard_map/ppermute | solution.py:418
